TPU v7x, 32 devices: a whole 2x2x4 slice. The times are simulated.
32 devices in a mesh: dom: 16 (over z, y, x), col: 2 (over core).
Axes of the slice: x: 2, y: 2, z: 4, core: 2. Of those that a mesh axis runs over, the one named last changes fastest.
Arguments:
- features: bfloat16 [16384, 256], P(('dom', 'col')), may hold values from -6 to 6
- weight: bfloat16 [256, 256], replicated, may hold values from -0.375 to 0.375
- cotangent: bfloat16 [16384, 256], P(('dom', 'col')), may hold values from -6 to 6
- tile_values: bfloat16 [1280, 128, 128], P(('dom', 'col')), may hold values from -0.15625 to 0.15625
- tile_rows: int32 [1280], P(('dom', 'col')), may hold values from 0 to 7
- tile_cols: int32 [1280], P(('dom', 'col')), may hold values from 0 to 19, as said below
- tile_count: int32 [32], P(('dom', 'col')), may hold values from 20 to 40, as said below
- send_blocks: int32 [32, 16], P(('dom', 'col')), may hold values from 0 to 3
Outputs:
- output_rows: bfloat16 [16384, 256], P(('dom', 'col'))
- feature_grad: bfloat16 [16384, 256], P(('dom', 'col'))
- weight_grad: float32 [256, 256], replicated
Inputs may be any that keep to these rules, and one draw needn't show every extreme that they name: `tile_cols`: A value v below 4 names the device's own row block v; a value 4 + s names the row block that the device of partition s with the same col index sends to this partition; no receive slot is named by two tiles of one device. Only the first tile_count slots of a device's tiles are live; some device has all 40 live.
All inputs are finite; a program needn't handle non-finite values.
Results may differ from a plain program's by a relative error of at most 0.0049.
Values may be sent and summed in bfloat16 or wider, within the bound.
A program may use at most 128 MiB of HBM per device.

v0:
```python
import functools

import jax
import jax.numpy as jnp
from jax import lax
from jax.experimental import pallas as pl
from jax.experimental.pallas import tpu as pltpu
from jax.sharding import PartitionSpec as P

MESH = pl.DeviceIdType.MESH
F32 = jnp.float32


def kernel(scale, rows_s, cols_s, count_s, send_s, feat_hbm, weight_hbm, cot_hbm, tiles_hbm,
           out, fgrad, wgrad,
           feat, weight, cot, tiles, sendf, recvf, sendb, recvb, buf, base, gh, psend, precv, hid,
           wsend, wrecv, wchunk, wpart, wall, wpeer, tos,
           f_send, f_recv, b_send, b_recv, r_send, r_recv, g_send, g_recv, misc):
    slots = tiles.shape[0]
    half, blk, width = feat.shape
    n = recvf.shape[0]
    blocks = 2 * half
    me = lax.axis_index("dom")
    col = lax.axis_index("col")
    other = 1 - col
    count = count_s[0]

    side = n // 2
    mine_side, spot = lax.div(me, side), lax.rem(me, side)

    def peer_side(k):
        return lax.rem(mine_side + 1 + lax.div(k - 1, side), 2) * side

    def to_peer(k):
        return peer_side(k) + lax.rem(spot + k, side)

    def from_peer(k):
        return peer_side(k) + lax.rem(spot + 2 * side - k, side)

    def remote(src, dst, s_sem, r_sem, dom, core):
        return pltpu.make_async_remote_copy(
            src_ref=src, dst_ref=dst, send_sem=s_sem, recv_sem=r_sem,
            device_id=(dom, core), device_id_type=MESH)

    feat_copy = pltpu.make_async_copy(feat_hbm, feat, misc.at[9])
    feat_copy.start()
    cot_copy = pltpu.make_async_copy(cot_hbm, cot, misc.at[10])
    cot_copy.start()
    weight_copy = pltpu.make_async_copy(weight_hbm, weight, misc.at[11])
    weight_copy.start()
    tile_copy = pltpu.make_async_copy(tiles_hbm, tiles, misc.at[0])
    tile_copy.start()

    barrier = pltpu.get_barrier_semaphore()

    def greet(k, carry):
        pl.semaphore_signal(barrier, inc=1, device_id=(to_peer(k), col), device_id_type=MESH)
        return carry

    lax.fori_loop(1, n, greet, 0)
    pl.semaphore_signal(barrier, inc=1, device_id=(me, other), device_id_type=MESH)

    feat_copy.wait()

    def gather(k, carry):
        sendf[k] = feat[send_s[to_peer(k)]]
        return carry

    lax.fori_loop(1, n, gather, 0)
    recvf[me] = feat[send_s[me]]

    cot_copy.wait()
    weight_copy.wait()
    own = lax.dot_general(cot[...], weight[...], (((1,), (1,)), ((), ())),
                          preferred_element_type=F32).astype(jnp.bfloat16)
    gh[pl.ds(col * half, half)] = own.reshape(half, blk, width)

    def find(s, carry):
        found = jnp.int32(0)
        for t in range(slots):
            found = jnp.where((cols_s[t] == s + half) & (t < count), t + 1, found)
        tos[s] = found
        return carry

    lax.fori_loop(0, n, find, 0)

    pl.semaphore_wait(barrier, n)

    def f_copy(k, peer, slot):
        return remote(sendf.at[k], recvf.at[slot], f_send.at[k], f_recv.at[slot], peer, col)

    def b_copy(k, peer, slot):
        return remote(sendb.at[k], recvb.at[slot], b_send.at[k], b_recv.at[slot], peer, col)

    gh_half = gh.at[pl.ds(col * half, half)]
    gh_copy = remote(gh_half, gh_half, misc.at[1], misc.at[2], me, other)
    gh_copy.start()

    def f_start(k, carry):
        f_copy(k, to_peer(k), me).start()
        return carry

    lax.fori_loop(1, n, f_start, 0)

    buf[0] = jnp.zeros((blk, width), F32)
    tile_copy.wait()
    gh_copy.wait_send()
    gh_other = gh.at[pl.ds(other * half, half)]
    remote(gh_other, gh_other, misc.at[1], misc.at[2], me, other).wait_recv()

    def back_term(slot):
        found = tos[slot]
        at = jnp.maximum(found - 1, 0)
        term = lax.dot_general(tiles[at], gh[rows_s[at]], (((0,), (0,)), ((), ())),
                               preferred_element_type=F32)
        return jnp.where(found > 0, term, 0.0).astype(jnp.bfloat16)

    def b_fill(k, carry):
        sendb[k] = back_term(to_peer(k))
        return carry

    lax.fori_loop(1, n, b_fill, 0)

    def b_start(k, carry):
        b_copy(k, to_peer(k), me).start()
        return carry

    cut1, cut2 = 1 + side // 2, 1 + 3 * side // 4
    ends = (1, cut1, cut2, side + 1)
    side_ends = (side + 1, side + side // 2, side + 3 * side // 4, n)

    def b_part(i):
        lax.fori_loop(ends[i], ends[i + 1], b_start, 0)
        lax.fori_loop(side_ends[i], side_ends[i + 1], b_start, 0)

    recvb[me] = back_term(me)

    def link(lasts, key, index):
        prev = jnp.int32(0)
        for r, last in enumerate(lasts):
            prev = jnp.where(key == r, last, prev)
        return prev, tuple(jnp.where(key == r, index, last) for r, last in enumerate(lasts))

    def own_back(t, lasts):
        key = jnp.where(t < count, cols_s[t], -1)
        prev, lasts = link(lasts, key, t + 1)
        term = lax.dot_general(tiles[t], gh[rows_s[t]], (((0,), (0,)), ((), ())),
                               preferred_element_type=F32)
        buf[t + 1] = buf[prev] + term
        return lasts

    lasts = lax.fori_loop(0, slots, own_back, (jnp.int32(0),) * half)
    for j in range(half):
        base[j] = buf[lasts[j]]

    def own_fwd(t, lasts):
        source = cols_s[t]
        key = jnp.where((t < count) & (source < half), rows_s[t], -1)
        prev, lasts = link(lasts, key, t + 1)
        term = jnp.dot(tiles[t], feat[jnp.minimum(source, half - 1)], preferred_element_type=F32)
        buf[t + 1] = buf[prev] + term
        return lasts

    lasts = lax.fori_loop(0, slots, own_fwd, (jnp.int32(0),) * blocks)

    b_part(0)

    def slot_fwd(k, slot, lasts):
        found = tos[slot]
        at = jnp.maximum(found - 1, 0)
        key = jnp.where(found > 0, rows_s[at], -1)
        prev, lasts = link(lasts, key, slots + 1 + k)
        term = jnp.dot(tiles[at], recvf[slot], preferred_element_type=F32)
        buf[slots + 1 + k] = buf[prev] + term
        return lasts

    lasts = slot_fwd(0, me, lasts)

    def arrived(i, lasts):
        k = n - i
        f_copy(k, from_peer(k), from_peer(k)).wait_recv()
        return slot_fwd(k, from_peer(k), lasts)

    lasts = lax.fori_loop(1, n, arrived, lasts)

    for j in range(half):
        psend[j] = buf[jnp.where(col == 0, lasts[half + j], lasts[j])]
    p_copy = remote(psend, precv, misc.at[3], misc.at[4], me, other)
    p_copy.start()
    p_copy.wait()
    for j in range(half):
        mine = buf[jnp.where(col == 0, lasts[j], lasts[half + j])]
        hid[pl.ds(j * blk, blk), :] = (mine + precv[j]).astype(jnp.bfloat16)

    local = lax.dot_general(hid[...], cot[...], (((0,), (0,)), ((), ())),
                            preferred_element_type=F32) * jnp.float32(scale)
    wh = width // 2
    low, high = local[:wh], local[wh:]
    wsend[...] = jnp.where(col == 0, high, low)
    w_copy = remote(wsend, wrecv, misc.at[5], misc.at[6], me, other)
    w_copy.start()
    out[...] = jnp.dot(hid[...], weight[...], preferred_element_type=F32).astype(jnp.bfloat16)
    w_copy.wait()
    share = jnp.where(col == 0, low, high) + wrecv[...]
    wchunk[...] = share.reshape(wchunk.shape)

    def r_copy(peer, chunk, slot):
        return remote(wchunk.at[chunk], wpart.at[slot], r_send.at[chunk], r_recv.at[slot], peer, col)

    def r_start(k, carry):
        r_copy(to_peer(k), to_peer(k), me).start()
        return carry

    lax.fori_loop(1, n, r_start, 0)
    b_part(1)
    wpart[me] = wchunk[me]

    def r_wait(k, carry):
        r_copy(from_peer(k), from_peer(k), from_peer(k)).wait_recv()
        return carry

    lax.fori_loop(1, n, r_wait, 0)
    wall[me] = jnp.sum(wpart[...], axis=0)

    def g_copy(k, peer, slot):
        return remote(wall.at[slot], wall.at[slot], g_send.at[k], g_recv.at[slot], peer, col)

    def g_start(k, carry):
        g_copy(k, to_peer(k), me).start()
        return carry

    lax.fori_loop(1, n, g_start, 0)
    b_part(2)

    def g_wait(k, carry):
        g_copy(k, from_peer(k), from_peer(k)).wait_recv()
        return carry

    lax.fori_loop(1, n, g_wait, 0)
    x_copy = remote(wall, wpeer, misc.at[7], misc.at[8], me, other)
    x_copy.start()
    wgrad[pl.ds(pl.multiple_of(col * wh, wh), wh), :] = wall[...].reshape(wh, wgrad.shape[1])

    def b_wait(k, carry):
        b_copy(k, from_peer(k), from_peer(k)).wait_recv()
        return carry

    lax.fori_loop(1, n, b_wait, 0)
    step = 16

    def total(i, carry):
        at = pl.ds(pl.multiple_of(i * step, step), step)

        def add(s, sums):
            value = recvb[s, at, :].astype(F32)
            home = send_s[s]
            return tuple(acc + jnp.where(home == j, value, 0.0) for j, acc in enumerate(sums))

        sums = lax.fori_loop(0, n, add, tuple(base[j, at, :] for j in range(half)), unroll=4)
        for j in range(half):
            fgrad[j, at, :] = sums[j].astype(jnp.bfloat16)
        return carry

    lax.fori_loop(0, blk // step, total, 0)

    def drain(k, carry):
        f_copy(k, to_peer(k), me).wait_send()
        b_copy(k, to_peer(k), me).wait_send()
        r_copy(to_peer(k), to_peer(k), me).wait_send()
        g_copy(k, to_peer(k), me).wait_send()
        return carry

    lax.fori_loop(1, n, drain, 0)
    x_copy.wait()
    wgrad[pl.ds(pl.multiple_of(other * wh, wh), wh), :] = wpeer[...].reshape(wh, wgrad.shape[1])


def place(*refs):
    count = (len(refs) - 1) // 3
    sources, targets, held, sem = refs[:count], refs[count:2 * count], refs[2 * count:-1], refs[-1]
    reads = [pltpu.make_async_copy(a, h, sem.at[i]) for i, (a, h) in enumerate(zip(sources, held))]
    writes = [pltpu.make_async_copy(h, b, sem.at[count + i]) for i, (h, b) in enumerate(zip(held, targets))]
    for read in reads:
        read.start()
    for read, write in zip(reads, writes):
        read.wait()
        write.start()
    for write in writes:
        write.wait()


def finish(*arrays):
    hbm = pl.BlockSpec(memory_space=pl.ANY)
    return pl.pallas_call(
        place,
        out_shape=tuple(jax.ShapeDtypeStruct(a.shape, a.dtype) for a in arrays),
        in_specs=[hbm] * len(arrays),
        out_specs=(hbm,) * len(arrays),
        scratch_shapes=[pltpu.VMEM(a.shape, a.dtype) for a in arrays]
        + [pltpu.SemaphoreType.DMA((2 * len(arrays),))],
    )(*arrays)


def local(features, weight, cotangent, tile_values, tile_rows, tile_cols, tile_count, send_blocks):
    slots, blk, _ = tile_values.shape
    rows, width = features.shape
    width_out = cotangent.shape[1]
    half = rows // blk
    n = send_blocks.shape[1]
    nodes = rows * lax.axis_size("col") * lax.axis_size("dom")
    scale = 1.0 / nodes**0.5
    bf = jnp.bfloat16
    chunk = width // 2 // n
    vmem = pl.BlockSpec(memory_space=pltpu.VMEM)
    hbm = pl.BlockSpec(memory_space=pl.ANY)
    smem = pl.BlockSpec(memory_space=pltpu.SMEM)
    sems = pltpu.SemaphoreType.DMA
    out, fgrad, wgrad = pl.pallas_call(
        functools.partial(kernel, scale),
        out_shape=(
            jax.ShapeDtypeStruct((rows, width_out), bf),
            jax.ShapeDtypeStruct((half, blk, width), bf),
            jax.ShapeDtypeStruct((width, width_out), F32),
        ),
        in_specs=[smem] * 4 + [hbm] * 4,
        out_specs=(vmem, vmem, vmem),
        scratch_shapes=[
            pltpu.VMEM((half, blk, width), bf),
            pltpu.VMEM((width, width_out), bf),
            pltpu.VMEM((rows, width_out), bf),
            pltpu.VMEM((slots, blk, blk), bf),
            pltpu.VMEM((n, blk, width), bf),
            pltpu.VMEM((n, blk, width), bf),
            pltpu.VMEM((n, blk, width), bf),
            pltpu.VMEM((n, blk, width), bf),
            pltpu.VMEM((slots + 1 + n, blk, width), F32),
            pltpu.VMEM((half, blk, width), F32),
            pltpu.VMEM((2 * half, blk, width), bf),
            pltpu.VMEM((half, blk, width), F32),
            pltpu.VMEM((half, blk, width), F32),
            pltpu.VMEM((rows, width), bf),
            pltpu.VMEM((width // 2, width_out), F32),
            pltpu.VMEM((width // 2, width_out), F32),
            pltpu.VMEM((n, chunk, width_out), F32),
            pltpu.VMEM((n, chunk, width_out), F32),
            pltpu.VMEM((n, chunk, width_out), F32),
            pltpu.VMEM((n, chunk, width_out), F32),
            pltpu.SMEM((n,), jnp.int32),
        ] + [sems((n,))] * 8 + [sems((12,))],
        compiler_params=pltpu.CompilerParams(
            collective_id=0, has_side_effects=True, vmem_limit_bytes=67000000),
    )(tile_rows, tile_cols, tile_count, send_blocks.reshape(n),
      features.reshape(half, blk, width), weight, cotangent, tile_values)
    return finish(out, fgrad.reshape(rows, width), wgrad)


def solution(mesh):
    return jax.shard_map(
        local,
        mesh=mesh,
        in_specs=(
            P(("dom", "col"), None),
            P(),
            P(("dom", "col"), None),
            P(("dom", "col"), None, None),
            P(("dom", "col")),
            P(("dom", "col")),
            P(("dom", "col")),
            P(("dom", "col"), None),
        ),
        out_specs=(P(("dom", "col"), None), P(("dom", "col"), None), P()),
        check_vma=False,
    )
```

profile of v0, /device:TPU:0, one launch (start us, length us, event | category | flops | bytes accessed | tf_op | source)
XLA Modules:
  0.0 66.7 jit_solution(18354941132757374611)
XLA Ops:
  1.3 63.5 %shard_map.103 = (bf16[512,256]{1,0:T(8,128)(2,1)}, bf16[4,128,256]{2,1,0:T(8,128)(2,1)}, f32[256,256]{1,0:T(8,128)}) custom-call(s32[40]{0:T(128)} %rows_s.1, s32[40]{0:T(128)} %cols_s.1, s32[1]{0:T(128)S(6)} %copy.11.count_s, s32[16]{0:T(128)} %bitcast.5, bf16[4,128,256]{2,1,0:T(8,128)(2,1)} %bitcast.3, bf16[256,256]{1,0:T(8,128)(2,1)} %weight_hbm.1, ...), custom_call_target="tpu_custom_call" | custom-call | tf_op jit(solution)/shard_map/pallas_call | solution.py:318
  64.8 1.9 %shard_map.104 = (bf16[512,256]{1,0:T(8,128)(2,1)}, bf16[512,256]{1,0:T(8,128)(2,1)}, f32[256,256]{1,0:T(8,128)}) custom-call(bf16[512,256]{1,0:T(8,128)(2,1)} %get-tuple-element.6.refs_0_, bf16[512,256]{1,0:T(8,128)(2,1)} %bitcast.4, f32[256,256]{1,0:T(8,128)} %get-tuple-element.8.refs_2_), custom_call_target="tpu_custom_call" | custom-call | tf_op jit(solution)/shard_map/pallas_call | solution.py:294
where the time goes:
time: 66.8 us; the launch traced here: 66.7 us
  Pallas kernels  65.4 us (98%)
  between operations  1.29 us (2%)
    pallas_call x1, Pallas kernels, local(): pl.pallas_call(functools.partial(kernel, scale), out_shape=(jax.ShapeDtyp...  63.5 us
    pallas_call x1, Pallas kernels, finish(): pl.pallas_call(place, out_shape=tuple((jax.ShapeDtypeStruct(a.shape, a.dt...  1.88 us

commit v1 on v0

--- a/solution.py
+++ b/solution.py
@@ -9,21 +9,29 @@
 
 MESH = pl.DeviceIdType.MESH
 F32 = jnp.float32
+BF16 = jnp.bfloat16
+Q = 4
 
 
 def kernel(scale, rows_s, cols_s, count_s, send_s, feat_hbm, weight_hbm, cot_hbm, tiles_hbm,
            out, fgrad, wgrad,
-           feat, weight, cot, tiles, sendf, recvf, sendb, recvb, buf, base, gh, psend, precv, hid,
-           wsend, wrecv, wchunk, wpart, wall, wpeer, tos,
-           f_send, f_recv, b_send, b_recv, r_send, r_recv, g_send, g_recv, misc):
+           feat, weight, cot, tiles, sendf, recvf, sendb, recvb, gin, buf, base, gh, psend, precv, hid,
+           wsend, wrecv, wchunk, wpart, wall, wpeer, tos, table, *rest):
+    lines = rest[:2 * (Q - 1)]
+    (t_send, t_recv, lf_send, lf_recv, s_send, s_recv, pf_send, pf_recv, pb_send, pb_recv,
+     r_send, r_recv, g_send, g_recv, misc) = rest[2 * (Q - 1):]
     slots = tiles.shape[0]
     half, blk, width = feat.shape
-    n = recvf.shape[0]
+    plane = recvf.shape[1]
+    n = Q * plane
     blocks = 2 * half
+    top = Q - 1
     me = lax.axis_index("dom")
     col = lax.axis_index("col")
     other = 1 - col
     count = count_s[0]
+    z, w = lax.div(me, plane), lax.rem(me, plane)
+    below = (z, top - z)
 
     side = n // 2
     mine_side, spot = lax.div(me, side), lax.rem(me, side)
@@ -60,19 +68,47 @@
     lax.fori_loop(1, n, greet, 0)
     pl.semaphore_signal(barrier, inc=1, device_id=(me, other), device_id_type=MESH)
 
+    gin[...] = jnp.zeros(gin.shape, gin.dtype)
+    buf[0] = jnp.zeros((blk, width), F32)
+
+    def keep(i, carry):
+        table[z, i] = send_s[i]
+        return carry
+
+    lax.fori_loop(0, n, keep, 0)
+
+    def pf_copy(s, peer, slot):
+        return remote(sendf.at[s, peer], recvf.at[s, slot], pf_send.at[s, peer], pf_recv.at[s, slot],
+                      z * plane + peer, col)
+
+    def pb_copy(s, peer, slot):
+        return remote(sendb.at[s, peer], recvb.at[s, slot], pb_send.at[s, peer], pb_recv.at[s, slot],
+                      z * plane + peer, col)
+
+    def peers(body):
+        def step(k, carry):
+            body(lax.rem(w + k, plane))
+            return carry
+
+        lax.fori_loop(1, plane, step, 0)
+
+    def pick(source, s):
+        def one(peer):
+            sendf[s, peer] = source[table[s, z * plane + peer]]
+
+        peers(one)
+        recvf[s, w] = source[table[s, me]]
+
+    def spread(s):
+        peers(lambda peer: pf_copy(s, peer, w).start())
+
     feat_copy.wait()
-
-    def gather(k, carry):
-        sendf[k] = feat[send_s[to_peer(k)]]
-        return carry
-
-    lax.fori_loop(1, n, gather, 0)
-    recvf[me] = feat[send_s[me]]
+    pick(feat, z)
 
     cot_copy.wait()
     weight_copy.wait()
     own = lax.dot_general(cot[...], weight[...], (((1,), (1,)), ((), ())),
-                          preferred_element_type=F32).astype(jnp.bfloat16)
+                          preferred_element_type=F32).astype(BF16)
     gh[pl.ds(col * half, half)] = own.reshape(half, blk, width)
 
     def find(s, carry):
@@ -86,23 +122,40 @@
 
     pl.semaphore_wait(barrier, n)
 
-    def f_copy(k, peer, slot):
-        return remote(sendf.at[k], recvf.at[slot], f_send.at[k], f_recv.at[slot], peer, col)
-
-    def b_copy(k, peer, slot):
-        return remote(sendb.at[k], recvb.at[slot], b_send.at[k], b_recv.at[slot], peer, col)
+    def held(d, k):
+        return feat if k == 0 else lines[d * top + k - 1]
+
+    def lf_copy(d, k, j):
+        nxt = z + 1 if d == 0 else z - 1
+        return remote(held(d, k).at[j], held(d, k + 1).at[j], lf_send.at[d, k, j], lf_recv.at[d, k, j],
+                      nxt * plane + w, col)
+
+    def s_copy(d, s, j):
+        nxt = z + 1 if d == 0 else z - 1
+        slot = s if d == 0 else jnp.where(s == nxt, Q, s)
+        return remote(gin.at[s, j], gin.at[slot, j], s_send.at[s, j], s_recv.at[slot, j],
+                      nxt * plane + w, col)
+
+    def line(k):
+        return lax.rem(z + k, Q)
+
+    def t_copy(k, slot):
+        return remote(send_s, table.at[slot], t_send.at[k], t_recv.at[slot], line(k) * plane + w, col)
+
+    for j in range(half):
+        for d in range(2):
+            @pl.when(below[d] < top)
+            def _():
+                lf_copy(d, 0, j).start()
+
+    for k in range(1, Q):
+        t_copy(k, z).start()
+    spread(z)
 
     gh_half = gh.at[pl.ds(col * half, half)]
     gh_copy = remote(gh_half, gh_half, misc.at[1], misc.at[2], me, other)
     gh_copy.start()
 
-    def f_start(k, carry):
-        f_copy(k, to_peer(k), me).start()
-        return carry
-
-    lax.fori_loop(1, n, f_start, 0)
-
-    buf[0] = jnp.zeros((blk, width), F32)
     tile_copy.wait()
     gh_copy.wait_send()
     gh_other = gh.at[pl.ds(other * half, half)]
@@ -113,27 +166,21 @@
         at = jnp.maximum(found - 1, 0)
         term = lax.dot_general(tiles[at], gh[rows_s[at]], (((0,), (0,)), ((), ())),
                                preferred_element_type=F32)
-        return jnp.where(found > 0, term, 0.0).astype(jnp.bfloat16)
-
-    def b_fill(k, carry):
-        sendb[k] = back_term(to_peer(k))
-        return carry
-
-    lax.fori_loop(1, n, b_fill, 0)
-
-    def b_start(k, carry):
-        b_copy(k, to_peer(k), me).start()
-        return carry
-
-    cut1, cut2 = 1 + side // 2, 1 + 3 * side // 4
-    ends = (1, cut1, cut2, side + 1)
-    side_ends = (side + 1, side + side // 2, side + 3 * side // 4, n)
-
-    def b_part(i):
-        lax.fori_loop(ends[i], ends[i + 1], b_start, 0)
-        lax.fori_loop(side_ends[i], side_ends[i + 1], b_start, 0)
-
-    recvb[me] = back_term(me)
+        return jnp.where(found > 0, term, 0.0).astype(BF16)
+
+    low_side = lax.div(z, Q // 2)
+    far = top * (1 - low_side)
+    near = 2 - low_side
+    pair = z + 1 - 2 * lax.rem(z, 2)
+    for s in (far, near, pair, z):
+        def fill(k, carry, s=s):
+            peer = lax.rem(w + k, plane)
+            sendb[s, peer] = back_term(s * plane + peer)
+            return carry
+
+        lax.fori_loop(0, plane, fill, 0, unroll=4)
+        recvb[s, w] = sendb[s, w]
+        peers(lambda peer, s=s: pb_copy(s, peer, w).start())
 
     def link(lasts, key, index):
         prev = jnp.int32(0)
@@ -149,7 +196,8 @@
         buf[t + 1] = buf[prev] + term
         return lasts
 
-    lasts = lax.fori_loop(0, slots, own_back, (jnp.int32(0),) * half)
+    unroll = 4 if slots % 4 == 0 else 1
+    lasts = lax.fori_loop(0, slots, own_back, (jnp.int32(0),) * half, unroll=unroll)
     for j in range(half):
         base[j] = buf[lasts[j]]
 
@@ -161,27 +209,99 @@
         buf[t + 1] = buf[prev] + term
         return lasts
 
-    lasts = lax.fori_loop(0, slots, own_fwd, (jnp.int32(0),) * blocks)
-
-    b_part(0)
-
-    def slot_fwd(k, slot, lasts):
-        found = tos[slot]
-        at = jnp.maximum(found - 1, 0)
-        key = jnp.where(found > 0, rows_s[at], -1)
-        prev, lasts = link(lasts, key, slots + 1 + k)
-        term = jnp.dot(tiles[at], recvf[slot], preferred_element_type=F32)
-        buf[slots + 1 + k] = buf[prev] + term
-        return lasts
-
-    lasts = slot_fwd(0, me, lasts)
-
-    def arrived(i, lasts):
-        k = n - i
-        f_copy(k, from_peer(k), from_peer(k)).wait_recv()
-        return slot_fwd(k, from_peer(k), lasts)
-
-    lasts = lax.fori_loop(1, n, arrived, lasts)
+    def slot_group(g, lasts):
+        if g == 0:
+            s = z
+        else:
+            zm = z + low_side * (top - 2 * z)
+            rel = g - 1 + jnp.where(g <= zm, 0, 1)
+            s = rel + low_side * (top - 2 * rel)
+        peers(lambda peer: pf_copy(s, peer, peer).wait_recv())
+
+        def step(k, lasts):
+            slot = lax.rem(w + k, plane)
+            found = tos[s * plane + slot]
+            at = jnp.maximum(found - 1, 0)
+            key = jnp.where(found > 0, rows_s[at], -1)
+            index = slots + 1 + g * plane + k
+            prev, lasts = link(lasts, key, index)
+            term = jnp.dot(tiles[at], recvf[s, slot], preferred_element_type=F32)
+            buf[index] = buf[prev] + term
+            return lasts
+
+        return lax.fori_loop(0, plane, step, lasts, unroll=4)
+
+    span = 64
+
+    def add_terms(s, j):
+        def rows(i, carry):
+            at = pl.ds(pl.multiple_of(i * span, span), span)
+
+            def add(slot, acc):
+                value = recvb[s, slot, at, :].astype(F32)
+                return acc + jnp.where(table[s, z * plane + slot] == j, value, 0.0)
+
+            acc = lax.fori_loop(0, plane, add, gin[s, j, at, :].astype(F32), unroll=4)
+            gin[s, j, at, :] = acc.astype(BF16)
+            return carry
+
+        lax.fori_loop(0, blk // span, rows, 0)
+
+    def sum_of(k, d):
+        rel = top - (k - below[d])
+        return rel if d == 0 else top - rel
+
+    def feat_of(k, d):
+        rel = below[d] - 1 - k
+        return rel if d == 0 else top - rel
+
+    def line_step(k):
+        for d in range(2):
+            @pl.when(below[d] <= k)
+            def _():
+                peers(lambda peer: pb_copy(sum_of(k, d), peer, peer).wait_recv())
+
+        def chunk(j, carry):
+            for d in range(2):
+                @pl.when(k < below[d])
+                def _():
+                    lf_copy(d, k, j).wait_recv()
+
+                    if k + 1 < top:
+                        @pl.when(below[d] < top)
+                        def _():
+                            lf_copy(d, k + 1, j).start()
+
+            for d in range(2):
+                @pl.when(below[d] <= k)
+                def _():
+                    s = sum_of(k, d)
+
+                    @pl.when(below[d] > 0)
+                    def _():
+                        remote(gin.at[s, j], gin.at[s, j], s_send.at[s, j], s_recv.at[s, j], me, other).wait_recv()
+
+                    add_terms(s, j)
+                    s_copy(d, s, j).start()
+            return carry
+
+        lax.fori_loop(0, half, chunk, 0)
+        for d in range(2):
+            @pl.when(k < below[d])
+            def _():
+                pick(held(d, k + 1), feat_of(k, d))
+                spread(feat_of(k, d))
+
+    for k in range(1, Q):
+        t_copy(k, line(k)).wait_recv()
+
+    line_step(0)
+    lasts = lax.fori_loop(0, slots, own_fwd, (jnp.int32(0),) * blocks, unroll=unroll)
+    lasts = slot_group(0, lasts)
+    for k in range(1, Q - 1):
+        line_step(k)
+        lasts = slot_group(k, lasts)
+    lasts = slot_group(Q - 1, lasts)
 
     for j in range(half):
         psend[j] = buf[jnp.where(col == 0, lasts[half + j], lasts[j])]
@@ -212,7 +332,6 @@
         return carry
 
     lax.fori_loop(1, n, r_start, 0)
-    b_part(1)
     wpart[me] = wchunk[me]
 
     def r_wait(k, carry):
@@ -230,7 +349,6 @@
         return carry
 
     lax.fori_loop(1, n, g_start, 0)
-    b_part(2)
 
     def g_wait(k, carry):
         g_copy(k, from_peer(k), from_peer(k)).wait_recv()
@@ -241,31 +359,60 @@
     x_copy.start()
     wgrad[pl.ds(pl.multiple_of(col * wh, wh), wh), :] = wall[...].reshape(wh, wgrad.shape[1])
 
-    def b_wait(k, carry):
-        b_copy(k, from_peer(k), from_peer(k)).wait_recv()
-        return carry
-
-    lax.fori_loop(1, n, b_wait, 0)
+    peers(lambda peer: pb_copy(z, peer, peer).wait_recv())
+
+    def sums_in(j, carry):
+        for d in range(2):
+            @pl.when(below[d] > 0)
+            def _():
+                slot = z if d == 0 else Q
+                remote(gin.at[slot, j], gin.at[slot, j], s_send.at[z, j], s_recv.at[slot, j], me, other).wait_recv()
+        return carry
+
+    lax.fori_loop(0, half, sums_in, 0)
     step = 16
 
     def total(i, carry):
         at = pl.ds(pl.multiple_of(i * step, step), step)
 
-        def add(s, sums):
-            value = recvb[s, at, :].astype(F32)
-            home = send_s[s]
+        def add(slot, sums):
+            value = recvb[z, slot, at, :].astype(F32)
+            home = send_s[z * plane + slot]
             return tuple(acc + jnp.where(home == j, value, 0.0) for j, acc in enumerate(sums))
 
-        sums = lax.fori_loop(0, n, add, tuple(base[j, at, :] for j in range(half)), unroll=4)
+        start = tuple(base[j, at, :] + gin[z, j, at, :].astype(F32) + gin[Q, j, at, :].astype(F32)
+                      for j in range(half))
+        sums = lax.fori_loop(0, plane, add, start, unroll=4)
         for j in range(half):
-            fgrad[j, at, :] = sums[j].astype(jnp.bfloat16)
+            fgrad[j, at, :] = sums[j].astype(BF16)
         return carry
 
     lax.fori_loop(0, blk // step, total, 0)
 
+    for k in range(1, Q):
+        t_copy(k, z).wait_send()
+    for s in range(Q):
+        def sent(peer, s=s):
+            pf_copy(s, peer, w).wait_send()
+            pb_copy(s, peer, w).wait_send()
+
+        peers(sent)
+
+    def line_sent(j, carry):
+        for d in range(2):
+            for k in range(Q - 1):
+                @pl.when((k <= below[d]) & (below[d] < top))
+                def _():
+                    lf_copy(d, k, j).wait_send()
+            for k in range(Q - 1):
+                @pl.when(below[d] <= k)
+                def _():
+                    s_copy(d, sum_of(k, d), j).wait_send()
+        return carry
+
+    lax.fori_loop(0, half, line_sent, 0)
+
     def drain(k, carry):
-        f_copy(k, to_peer(k), me).wait_send()
-        b_copy(k, to_peer(k), me).wait_send()
         r_copy(to_peer(k), to_peer(k), me).wait_send()
         g_copy(k, to_peer(k), me).wait_send()
         return carry
@@ -307,6 +454,7 @@
     width_out = cotangent.shape[1]
     half = rows // blk
     n = send_blocks.shape[1]
+    plane = n // Q
     nodes = rows * lax.axis_size("col") * lax.axis_size("dom")
     scale = 1.0 / nodes**0.5
     bf = jnp.bfloat16
@@ -329,10 +477,11 @@
             pltpu.VMEM((width, width_out), bf),
             pltpu.VMEM((rows, width_out), bf),
             pltpu.VMEM((slots, blk, blk), bf),
-            pltpu.VMEM((n, blk, width), bf),
-            pltpu.VMEM((n, blk, width), bf),
-            pltpu.VMEM((n, blk, width), bf),
-            pltpu.VMEM((n, blk, width), bf),
+            pltpu.VMEM((Q, plane, blk, width), bf),
+            pltpu.VMEM((Q, plane, blk, width), bf),
+            pltpu.VMEM((Q, plane, blk, width), bf),
+            pltpu.VMEM((Q, plane, blk, width), bf),
+            pltpu.VMEM((Q + 1, half, blk, width), bf),
             pltpu.VMEM((slots + 1 + n, blk, width), F32),
             pltpu.VMEM((half, blk, width), F32),
             pltpu.VMEM((2 * half, blk, width), bf),
@@ -346,7 +495,12 @@
             pltpu.VMEM((n, chunk, width_out), F32),
             pltpu.VMEM((n, chunk, width_out), F32),
             pltpu.SMEM((n,), jnp.int32),
-        ] + [sems((n,))] * 8 + [sems((12,))],
+            pltpu.SMEM((Q, n), jnp.int32),
+        ] + [pltpu.VMEM((half, blk, width), bf)] * (2 * (Q - 1)) + [
+            sems((Q,)), sems((Q,)),
+            sems((2, Q - 1, half)), sems((2, Q - 1, half)),
+            sems((Q, half)), sems((Q + 1, half)),
+        ] + [sems((Q, plane))] * 4 + [sems((n,))] * 4 + [sems((12,))],
         compiler_params=pltpu.CompilerParams(
             collective_id=0, has_side_effects=True, vmem_limit_bytes=67000000),
     )(tile_rows, tile_cols, tile_count, send_blocks.reshape(n),

time: 66.8 us -> 53 us (0.79)
  Pallas kernels: 65.4 us -> 51.6 us
    pallas_call x1, Pallas kernels: 63.5 us -> 49.7 us  [local(): pl.pallas_call(functools.partial(kernel, scale), out_shape=(jax.ShapeDtyp...]
where the time goes in v1:
time: 53 us; the launch traced here: 52.9 us
  Pallas kernels  51.6 us (97%)
  between operations  1.29 us (2%)
    pallas_call x1, Pallas kernels, local(): pl.pallas_call(functools.partial(kernel, scale), out_shape=(jax.ShapeDtyp...  49.7 us
    pallas_call x1, Pallas kernels, finish(): pl.pallas_call(place, out_shape=tuple((jax.ShapeDtypeStruct(a.shape, a.dt...  1.88 us

profile of v1, /device:TPU:0, one launch (start us, length us, event | category | flops | bytes accessed | tf_op | source)
XLA Modules:
  0.0 52.9 jit_solution(12246082228171847717)
XLA Ops:
  1.3 49.7 %shard_map.103 = (bf16[512,256]{1,0:T(8,128)(2,1)}, bf16[4,128,256]{2,1,0:T(8,128)(2,1)}, f32[256,256]{1,0:T(8,128)}) custom-call(s32[40]{0:T(128)} %rows_s.1, s32[40]{0:T(128)} %cols_s.1, s32[1]{0:T(128)S(6)} %copy.11.count_s, s32[16]{0:T(128)} %bitcast.5, bf16[4,128,256]{2,1,0:T(8,128)(2,1)} %bitcast.3, bf16[256,256]{1,0:T(8,128)(2,1)} %weight_hbm.1, ...), custom_call_target="tpu_custom_call" | custom-call | tf_op jit(solution)/shard_map/pallas_call | solution.py:466
  51.0 1.9 %shard_map.104 = (bf16[512,256]{1,0:T(8,128)(2,1)}, bf16[512,256]{1,0:T(8,128)(2,1)}, f32[256,256]{1,0:T(8,128)}) custom-call(bf16[512,256]{1,0:T(8,128)(2,1)} %get-tuple-element.6.refs_0_, bf16[512,256]{1,0:T(8,128)(2,1)} %bitcast.4, f32[256,256]{1,0:T(8,128)} %get-tuple-element.8.refs_2_), custom_call_target="tpu_custom_call" | custom-call | tf_op jit(solution)/shard_map/pallas_call | solution.py:441

commit v2 on v1

v2 whole, which is shorter than its diff:
```python
import functools

import jax
import jax.numpy as jnp
from jax import lax
from jax.experimental import pallas as pl
from jax.experimental.pallas import tpu as pltpu
from jax.sharding import PartitionSpec as P

MESH = pl.DeviceIdType.MESH
F32 = jnp.float32
BF16 = jnp.bfloat16
Q = 4
CH = 4


def kernel(scale, owners, rows_s, cols_s, count_s, send_s, feat_hbm, weight_hbm, cot_hbm, tiles_hbm,
           out_hbm, fgrad_hbm, wgrad_hbm,
           feat, weight, cot, tiles, sendf, recvf, sendb, recvb, gin, buf, base, gh, psend, precv, hid,
           part, out, fgrad, wgrad, wchunk, wpart, wall, tos, table, *rest):
    lines = rest[:2 * (Q - 1) * CH]
    (t_send, t_recv, lf_send, lf_recv, s_send, s_recv, pf_send, pf_recv, pb_send, pb_recv,
     r_send, r_recv, g_send, g_recv, misc) = rest[2 * (Q - 1) * CH:]
    slots = tiles.shape[0]
    half, blk, width = feat.shape
    plane = recvf.shape[1]
    n = Q * plane
    blocks = 2 * half
    top = Q - 1
    tall = blk // CH
    me = lax.axis_index("dom")
    col = lax.axis_index("col")
    other = 1 - col
    count = count_s[0]
    z, w = lax.div(me, plane), lax.rem(me, plane)
    below = (z, top - z)
    flat = 2 * me + col

    def remote(src, dst, s_sem, r_sem, dom, core):
        return pltpu.make_async_remote_copy(
            src_ref=src, dst_ref=dst, send_sem=s_sem, recv_sem=r_sem,
            device_id=(dom, core), device_id_type=MESH)

    def line(k):
        return lax.rem(z + k, Q)

    def peers(body):
        def step(k, carry):
            body(lax.rem(w + k, plane))
            return carry

        lax.fori_loop(1, plane, step, 0)

    feat_copy = pltpu.make_async_copy(feat_hbm, feat, misc.at[0])
    feat_copy.start()
    barrier = pltpu.get_barrier_semaphore()

    def greet(dom, core):
        pl.semaphore_signal(barrier, inc=1, device_id=(dom, core), device_id_type=MESH)

    for k in range(1, Q):
        greet(line(k) * plane + w, col)
    peers(lambda peer: greet(z * plane + peer, col))
    greet(me, other)
    rows = half * blk
    cot_half = cot.at[pl.ds(pl.multiple_of(col * rows, rows), rows)]
    cot_copy = pltpu.make_async_copy(cot_hbm, cot_half, misc.at[1])
    cot_copy.start()
    weight_copy = pltpu.make_async_copy(weight_hbm, weight, misc.at[2])
    weight_copy.start()
    tile_copy = pltpu.make_async_copy(tiles_hbm, tiles, misc.at[3])
    tile_copy.start()

    gin[...] = jnp.zeros(gin.shape, gin.dtype)
    buf[0] = jnp.zeros((blk, width), F32)

    def keep(i, carry):
        table[z, i] = send_s[i]
        return carry

    lax.fori_loop(0, n, keep, 0)

    def part_of(c):
        return pl.ds(c * tall, tall)

    def pf_copy(s, peer, slot, at):
        return remote(sendf.at[s, peer, at], recvf.at[s, slot, at], pf_send.at[s, peer], pf_recv.at[s, slot],
                      z * plane + peer, col)

    def pb_copy(s, peer, slot):
        return remote(sendb.at[s, peer], recvb.at[s, slot], pb_send.at[s, peer], pb_recv.at[s, slot],
                      z * plane + peer, col)

    whole = pl.ds(0, blk)

    def spread(source, s, at):
        def one(peer):
            sendf[s, peer, at, :] = source[table[s, z * plane + peer]]

        peers(one)
        peers(lambda peer: pf_copy(s, peer, w, at).start())
        recvf[s, w, at, :] = source[table[s, me]]

    def lf_copy(d, k, c):
        nxt = z + 1 if d == 0 else z - 1
        src = feat.at[:, part_of(c)] if k == 0 else lines[(d * top + k - 1) * CH + c]
        return remote(src, lines[(d * top + k) * CH + c], lf_send.at[d, k, c], lf_recv.at[d, k, c],
                      nxt * plane + w, col)

    def s_copy(d, s, c):
        nxt = z + 1 if d == 0 else z - 1
        slot = s if d == 0 else jnp.where(s == nxt, Q, s)
        return remote(gin.at[s, :, part_of(c)], gin.at[slot, :, part_of(c)], s_send.at[s, c], s_recv.at[slot, c],
                      nxt * plane + w, col)

    def s_wait(slot, c):
        remote(gin.at[slot, :, part_of(c)], gin.at[slot, :, part_of(c)], s_send.at[0, c], s_recv.at[slot, c],
               me, other).wait_recv()

    def t_copy(k, slot):
        return remote(send_s, table.at[slot], t_send.at[k], t_recv.at[slot], line(k) * plane + w, col)

    feat_copy.wait()
    pl.semaphore_wait(barrier, top + plane)

    for k in range(1, Q):
        t_copy(k, z).start()
    for c in range(CH):
        for d in range(2):
            @pl.when(below[d] < top)
            def _():
                lf_copy(d, 0, c).start()

    spread(feat, z, whole)
    cot_copy.wait()
    c_copy = remote(cot_half, cot_half, misc.at[4], misc.at[5], me, other)
    c_copy.start()

    def find(s, carry):
        found = jnp.int32(0)
        for t in range(slots):
            found = jnp.where((cols_s[t] == s + half) & (t < count), t + 1, found)
        tos[s] = found
        return carry

    lax.fori_loop(0, n, find, 0)
    weight_copy.wait()
    cot_other = cot.at[pl.ds(pl.multiple_of(other * rows, rows), rows)]
    remote(cot_other, cot_other, misc.at[4], misc.at[5], me, other).wait_recv()
    gh[...] = lax.dot_general(cot[...], weight[...], (((1,), (1,)), ((), ())),
                              preferred_element_type=F32).astype(BF16).reshape(gh.shape)
    tile_copy.wait()

    def back_term(slot):
        found = tos[slot]
        at = jnp.maximum(found - 1, 0)
        term = lax.dot_general(tiles[at], gh[rows_s[at]], (((0,), (0,)), ((), ())),
                               preferred_element_type=F32)
        return jnp.where(found > 0, term, 0.0).astype(BF16)

    def back_send(s):
        peers(lambda peer: pb_copy(s, peer, w).start())

    low_side = lax.div(z, Q // 2)
    far = top * (1 - low_side)
    near = 2 - low_side
    pair = z + 1 - 2 * lax.rem(z, 2)
    for i, s in enumerate((far, near, pair, z)):
        def fill(k, carry, s=s):
            peer = lax.rem(w + k, plane)
            sendb[s, peer] = back_term(s * plane + peer)
            return carry

        lax.fori_loop(0, plane, fill, 0, unroll=4)
        recvb[s, w] = sendb[s, w]
        if i < top:
            back_send(s)

    def link(lasts, key, index):
        prev = jnp.int32(0)
        for r, last in enumerate(lasts):
            prev = jnp.where(key == r, last, prev)
        return prev, tuple(jnp.where(key == r, index, last) for r, last in enumerate(lasts))

    def own_back(t, lasts):
        key = jnp.where(t < count, cols_s[t], -1)
        prev, lasts = link(lasts, key, t + 1)
        term = lax.dot_general(tiles[t], gh[rows_s[t]], (((0,), (0,)), ((), ())),
                               preferred_element_type=F32)
        buf[t + 1] = buf[prev] + term
        return lasts

    unroll = 4 if slots % 4 == 0 else 1

    def own_fwd(t, lasts):
        source = cols_s[t]
        key = jnp.where((t < count) & (source < half), rows_s[t], -1)
        prev, lasts = link(lasts, key, t + 1)
        term = jnp.dot(tiles[t], feat[jnp.minimum(source, half - 1)], preferred_element_type=F32)
        buf[t + 1] = buf[prev] + term
        return lasts

    def slot_group(g, lasts):
        if g == 0:
            s = z
        else:
            zm = z + low_side * (top - 2 * z)
            rel = g - 1 + jnp.where(g <= zm, 0, 1)
            s = rel + low_side * (top - 2 * rel)
        peers(lambda peer: pf_copy(s, peer, peer, whole).wait_recv())

        def step(k, lasts):
            slot = lax.rem(w + k, plane)
            found = tos[s * plane + slot]
            at = jnp.maximum(found - 1, 0)
            key = jnp.where(found > 0, rows_s[at], -1)
            index = slots + 1 + g * plane + k
            prev, lasts = link(lasts, key, index)
            term = jnp.dot(tiles[at], recvf[s, slot], preferred_element_type=F32)
            buf[index] = buf[prev] + term
            return lasts

        return lax.fori_loop(0, plane, step, lasts, unroll=4)

    def sums(s, at, starts):
        def add(slot, accs):
            value = recvb[s, slot, at, :].astype(F32)
            home = table[s, z * plane + slot]
            return tuple(acc + jnp.where(home == j, value, 0.0) for j, acc in enumerate(accs))

        return lax.fori_loop(0, plane, add, starts, unroll=4)

    def sum_of(k, d):
        rel = top - (k - below[d])
        return rel if d == 0 else top - rel

    def feat_of(k, d):
        rel = below[d] - 1 - k
        return rel if d == 0 else top - rel

    def feats(k):
        for c in range(CH):
            for d in range(2):
                @pl.when(k < below[d])
                def _():
                    lf_copy(d, k, c).wait_recv()

                    if k + 1 < top:
                        @pl.when(below[d] < top)
                        def _():
                            lf_copy(d, k + 1, c).start()

            for d in range(2):
                @pl.when(k < below[d])
                def _():
                    spread(lines[(d * top + k) * CH + c], feat_of(k, d), part_of(c))

    def grads(k):
        for d in range(2):
            @pl.when(below[d] <= k)
            def _():
                peers(lambda peer: pb_copy(sum_of(k, d), peer, peer).wait_recv())

        step = tall // 2
        for c in range(CH):
            for d in range(2):
                @pl.when(below[d] <= k)
                def _():
                    s = sum_of(k, d)

                    @pl.when(below[d] > 0)
                    def _():
                        s_wait(s, c)

                    def some(i, carry):
                        at = pl.ds(pl.multiple_of(c * tall + i * step, step), step)
                        accs = sums(s, at, tuple(gin[s, j, at, :].astype(F32) for j in range(half)))
                        for j in range(half):
                            gin[s, j, at, :] = accs[j].astype(BF16)
                        return carry

                    lax.fori_loop(0, tall // step, some, 0)
                    s_copy(d, s, c).start()

    for k in range(1, Q):
        t_copy(k, line(k)).wait_recv()

    feats(0)
    grads(0)
    lasts = lax.fori_loop(0, slots, own_back, (jnp.int32(0),) * half, unroll=unroll)
    for j in range(half):
        base[j] = buf[lasts[j]]
    feats(1)
    grads(1)
    lasts = lax.fori_loop(0, slots, own_fwd, (jnp.int32(0),) * blocks, unroll=unroll)
    lasts = slot_group(0, lasts)
    feats(2)
    back_send(z)
    grads(2)
    for g in range(1, Q):
        lasts = slot_group(g, lasts)

    for r in range(blocks):
        part[r * blk:(r + 1) * blk, :] = buf[lasts[r]].astype(BF16)
    for j in range(half):
        psend[j] = buf[jnp.where(col == 0, lasts[half + j], lasts[j])]
    p_copy = remote(psend, precv, misc.at[6], misc.at[7], me, other)
    p_copy.start()
    term = lax.dot_general(part[...], cot[...], (((0,), (0,)), ((), ())),
                           preferred_element_type=F32) * jnp.float32(scale)
    wchunk[...] = term.astype(BF16).reshape(wchunk.shape)

    first, doms = owners
    held = 2 * doms
    mine = flat - 2 * first
    is_owner = (me >= first) & (me < first + doms)

    def r_copy(o):
        return remote(wchunk.at[o], wpart.at[flat], r_send.at[o], r_recv.at[flat],
                      first + lax.div(o, 2), lax.rem(o, 2))

    def r_in(f):
        return remote(wchunk.at[0], wpart.at[f], r_send.at[0], r_recv.at[f], me, other)

    def others(limit, start, skip, body):
        def step(k, carry):
            at = lax.rem(start + k, limit)

            @pl.when(at != skip)
            def _():
                body(at)
            return carry

        lax.fori_loop(0, limit, step, 0)

    others(held, lax.rem(flat, held), mine, lambda o: r_copy(o).start())

    p_copy.wait()
    for j in range(half):
        whose = buf[jnp.where(col == 0, lasts[j], lasts[half + j])]
        hid[pl.ds(j * blk, blk), :] = (whose + precv[j]).astype(BF16)
    out[...] = jnp.dot(hid[...], weight[...], preferred_element_type=F32).astype(BF16)
    out_copy = pltpu.make_async_copy(out, out_hbm, misc.at[8])
    out_copy.start()

    def g_copy(f):
        return remote(wall.at[mine], wall.at[mine], g_send.at[f], g_recv.at[mine], lax.div(f, 2), lax.rem(f, 2))

    def g_in(o):
        return remote(wall.at[o], wall.at[o], g_send.at[0], g_recv.at[o], me, other)

    @pl.when(is_owner)
    def _():
        wpart[flat] = wchunk[mine]
        others(2 * n, flat, flat, lambda f: r_in(f).wait_recv())
        total = lax.fori_loop(0, 2 * n, lambda f, acc: acc + wpart[f].astype(F32),
                              jnp.zeros(wpart.shape[1:], F32), unroll=4)
        wall[mine] = total.astype(BF16)
        others(2 * n, flat, flat, lambda f: g_copy(f).start())

    peers(lambda peer: pb_copy(z, peer, peer).wait_recv())
    for c in range(CH):
        for d in range(2):
            @pl.when(below[d] > 0)
            def _():
                s_wait(z if d == 0 else Q, c)

    step = 16

    def final(i, carry):
        at = pl.ds(pl.multiple_of(i * step, step), step)
        starts = tuple(base[j, at, :] + gin[z, j, at, :].astype(F32) + gin[Q, j, at, :].astype(F32)
                       for j in range(half))
        accs = sums(z, at, starts)
        for j in range(half):
            fgrad[j, at, :] = accs[j].astype(BF16)
        return carry

    lax.fori_loop(0, blk // step, final, 0)
    fgrad_copy = pltpu.make_async_copy(fgrad, fgrad_hbm, misc.at[9])
    fgrad_copy.start()

    for k in range(1, Q):
        t_copy(k, z).wait_send()
    for s in range(Q):
        def sent(peer, s=s):
            pf_copy(s, peer, w, whole).wait_send()
            pb_copy(s, peer, w).wait_send()

        peers(sent)
    for c in range(CH):
        for d in range(2):
            for k in range(Q - 1):
                @pl.when((k <= below[d]) & (below[d] < top))
                def _():
                    lf_copy(d, k, c).wait_send()

                @pl.when(below[d] <= k)
                def _():
                    s_copy(d, sum_of(k, d), c).wait_send()
    c_copy.wait_send()
    others(held, 0, mine, lambda o: r_copy(o).wait_send())

    others(held, 0, mine, lambda o: g_in(o).wait_recv())
    wgrad[...] = wall[...].astype(F32).reshape(wgrad.shape)
    wgrad_copy = pltpu.make_async_copy(wgrad, wgrad_hbm, misc.at[10])
    wgrad_copy.start()

    @pl.when(is_owner)
    def _():
        others(2 * n, 0, flat, lambda f: g_copy(f).wait_send())

    out_copy.wait()
    fgrad_copy.wait()
    wgrad_copy.wait()


def place(*refs):
    count = (len(refs) - 1) // 3
    sources, targets, held, sem = refs[:count], refs[count:2 * count], refs[2 * count:-1], refs[-1]
    reads = [pltpu.make_async_copy(a, h, sem.at[i]) for i, (a, h) in enumerate(zip(sources, held))]
    writes = [pltpu.make_async_copy(h, b, sem.at[count + i]) for i, (h, b) in enumerate(zip(held, targets))]
    for read in reads:
        read.start()
    for read, write in zip(reads, writes):
        read.wait()
        write.start()
    for write in writes:
        write.wait()


def finish(*arrays):
    hbm = pl.BlockSpec(memory_space=pl.ANY)
    return pl.pallas_call(
        place,
        out_shape=tuple(jax.ShapeDtypeStruct(a.shape, a.dtype) for a in arrays),
        in_specs=[hbm] * len(arrays),
        out_specs=(hbm,) * len(arrays),
        scratch_shapes=[pltpu.VMEM(a.shape, a.dtype) for a in arrays]
        + [pltpu.SemaphoreType.DMA((2 * len(arrays),))],
    )(*arrays)


def local(features, weight, cotangent, tile_values, tile_rows, tile_cols, tile_count, send_blocks):
    slots, blk, _ = tile_values.shape
    rows, width = features.shape
    width_out = cotangent.shape[1]
    half = rows // blk
    n = send_blocks.shape[1]
    plane = n // Q
    nodes = rows * lax.axis_size("col") * lax.axis_size("dom")
    scale = 1.0 / nodes**0.5
    bf = jnp.bfloat16
    doms = min(n // 2, width // 16)
    owners = (n // 4, doms)
    chunk = width // (2 * doms)
    hbm = pl.BlockSpec(memory_space=pl.ANY)
    smem = pl.BlockSpec(memory_space=pltpu.SMEM)
    sems = pltpu.SemaphoreType.DMA
    out, fgrad, wgrad = pl.pallas_call(
        functools.partial(kernel, scale, owners),
        out_shape=(
            jax.ShapeDtypeStruct((rows, width_out), bf),
            jax.ShapeDtypeStruct((half, blk, width), bf),
            jax.ShapeDtypeStruct((width, width_out), F32),
        ),
        in_specs=[smem] * 4 + [hbm] * 4,
        out_specs=(hbm, hbm, hbm),
        scratch_shapes=[
            pltpu.VMEM((half, blk, width), bf),
            pltpu.VMEM((width, width_out), bf),
            pltpu.VMEM((2 * rows, width_out), bf),
            pltpu.VMEM((slots, blk, blk), bf),
            pltpu.VMEM((Q, plane, blk, width), bf),
            pltpu.VMEM((Q, plane, blk, width), bf),
            pltpu.VMEM((Q, plane, blk, width), bf),
            pltpu.VMEM((Q, plane, blk, width), bf),
            pltpu.VMEM((Q + 1, half, blk, width), bf),
            pltpu.VMEM((slots + 1 + n, blk, width), F32),
            pltpu.VMEM((half, blk, width), F32),
            pltpu.VMEM((2 * half, blk, width), bf),
            pltpu.VMEM((half, blk, width), F32),
            pltpu.VMEM((half, blk, width), F32),
            pltpu.VMEM((rows, width), bf),
            pltpu.VMEM((2 * rows, width), bf),
            pltpu.VMEM((rows, width_out), bf),
            pltpu.VMEM((half, blk, width), bf),
            pltpu.VMEM((width, width_out), F32),
            pltpu.VMEM((2 * doms, chunk, width_out), bf),
            pltpu.VMEM((2 * n, chunk, width_out), bf),
            pltpu.VMEM((2 * doms, chunk, width_out), bf),
            pltpu.SMEM((n,), jnp.int32),
            pltpu.SMEM((Q, n), jnp.int32),
        ] + [pltpu.VMEM((half, blk // CH, width), bf)] * (2 * (Q - 1) * CH) + [
            sems((Q,)), sems((Q,)),
            sems((2, Q - 1, CH)), sems((2, Q - 1, CH)),
            sems((Q, CH)), sems((Q + 1, CH)),
        ] + [sems((Q, plane))] * 4 + [
            sems((2 * doms,)), sems((2 * n,)), sems((2 * n,)), sems((2 * doms,)), sems((11,)),
        ],
        compiler_params=pltpu.CompilerParams(
            collective_id=0, has_side_effects=True, vmem_limit_bytes=67000000),
    )(tile_rows, tile_cols, tile_count, send_blocks.reshape(n),
      features.reshape(half, blk, width), weight, cotangent, tile_values)
    return finish(out, fgrad.reshape(rows, width), wgrad)


def solution(mesh):
    return jax.shard_map(
        local,
        mesh=mesh,
        in_specs=(
            P(("dom", "col"), None),
            P(),
            P(("dom", "col"), None),
            P(("dom", "col"), None, None),
            P(("dom", "col")),
            P(("dom", "col")),
            P(("dom", "col")),
            P(("dom", "col"), None),
        ),
        out_specs=(P(("dom", "col"), None), P(("dom", "col"), None), P()),
        check_vma=False,
    )
```

time: 53 us -> 47.5 us (0.90)
  Pallas kernels: 51.6 us -> 46 us
    pallas_call x1, Pallas kernels: 49.7 us -> 44.2 us  [local(): pl.pallas_call(functools.partial(kernel, scale, owners), out_shape=(jax.S...]
where the time goes in v2:
time: 47.5 us; the launch traced here: 47.3 us
  Pallas kernels  46 us (97%)
  between operations  1.29 us (3%)
    pallas_call x1, Pallas kernels, local(): pl.pallas_call(functools.partial(kernel, scale, owners), out_shape=(jax.S...  44.2 us
    pallas_call x1, Pallas kernels, finish(): pl.pallas_call(place, out_shape=tuple((jax.ShapeDtypeStruct(a.shape, a.dt...  1.88 us

profile of v2, /device:TPU:0, one launch (start us, length us, event | category | flops | bytes accessed | tf_op | source)
XLA Modules:
  0.0 47.3 jit_solution(12493889868083613218)
XLA Ops:
  1.3 44.2 %shard_map.103 = (bf16[512,256]{1,0:T(8,128)(2,1)}, bf16[4,128,256]{2,1,0:T(8,128)(2,1)}, f32[256,256]{1,0:T(8,128)}) custom-call(s32[40]{0:T(128)} %rows_s.1, s32[40]{0:T(128)} %cols_s.1, s32[1]{0:T(128)S(6)} %copy.11.count_s, s32[16]{0:T(128)} %bitcast.5, bf16[4,128,256]{2,1,0:T(8,128)(2,1)} %bitcast.3, bf16[256,256]{1,0:T(8,128)(2,1)} %weight_hbm.1, ...), custom_call_target="tpu_custom_call" | custom-call | tf_op jit(solution)/shard_map/pallas_call | solution.py:460
  45.4 1.9 %shard_map.104 = (bf16[512,256]{1,0:T(8,128)(2,1)}, bf16[512,256]{1,0:T(8,128)(2,1)}, f32[256,256]{1,0:T(8,128)}) custom-call(bf16[512,256]{1,0:T(8,128)(2,1)} %get-tuple-element.6.refs_0_, bf16[512,256]{1,0:T(8,128)(2,1)} %bitcast.4, f32[256,256]{1,0:T(8,128)} %get-tuple-element.8.refs_2_), custom_call_target="tpu_custom_call" | custom-call | tf_op jit(solution)/shard_map/pallas_call | solution.py:434

commit v3 on v2

--- a/solution.py
+++ b/solution.py
@@ -19,7 +19,7 @@
            feat, weight, cot, tiles, sendf, recvf, sendb, recvb, gin, buf, base, gh, psend, precv, hid,
            part, out, fgrad, wgrad, wchunk, wpart, wall, tos, table, *rest):
     lines = rest[:2 * (Q - 1) * CH]
-    (t_send, t_recv, lf_send, lf_recv, s_send, s_recv, pf_send, pf_recv, pb_send, pb_recv,
+    (t_send, t_recv, lf_send, s_send, l_recv, pf_send, pf_recv, pb_send, pb_recv,
      r_send, r_recv, g_send, g_recv, misc) = rest[2 * (Q - 1) * CH:]
     slots = tiles.shape[0]
     half, blk, width = feat.shape
@@ -84,14 +84,20 @@
         return pl.ds(c * tall, tall)
 
     def pf_copy(s, peer, slot, at):
-        return remote(sendf.at[s, peer, at], recvf.at[s, slot, at], pf_send.at[s, peer], pf_recv.at[s, slot],
+        return remote(sendf.at[s, peer, at], recvf.at[s, slot, at], pf_send, pf_recv.at[s],
                       z * plane + peer, col)
 
     def pb_copy(s, peer, slot):
-        return remote(sendb.at[s, peer], recvb.at[s, slot], pb_send.at[s, peer], pb_recv.at[s, slot],
+        return remote(sendb.at[s, peer], recvb.at[s, slot], pb_send, pb_recv.at[s],
                       z * plane + peer, col)
 
     whole = pl.ds(0, blk)
+
+    def done(ref, sem):
+        return remote(ref, ref, sem, sem, me, other)
+
+    def from_peers(buffer, sem, s):
+        done(buffer.at[s, pl.ds(0, plane - 1)], sem.at[s]).wait_recv()
 
     def spread(source, s, at):
         def one(peer):
@@ -104,21 +110,20 @@
     def lf_copy(d, k, c):
         nxt = z + 1 if d == 0 else z - 1
         src = feat.at[:, part_of(c)] if k == 0 else lines[(d * top + k - 1) * CH + c]
-        return remote(src, lines[(d * top + k) * CH + c], lf_send.at[d, k, c], lf_recv.at[d, k, c],
+        return remote(src, lines[(d * top + k) * CH + c], lf_send.at[d], l_recv.at[d, k, c],
                       nxt * plane + w, col)
 
-    def s_copy(d, s, c):
+    def s_copy(d, k, s, c):
         nxt = z + 1 if d == 0 else z - 1
         slot = s if d == 0 else jnp.where(s == nxt, Q, s)
-        return remote(gin.at[s, :, part_of(c)], gin.at[slot, :, part_of(c)], s_send.at[s, c], s_recv.at[slot, c],
+        return remote(gin.at[s, :, part_of(c)], gin.at[slot, :, part_of(c)], s_send.at[d], l_recv.at[d, k + 1, c],
                       nxt * plane + w, col)
 
-    def s_wait(slot, c):
-        remote(gin.at[slot, :, part_of(c)], gin.at[slot, :, part_of(c)], s_send.at[0, c], s_recv.at[slot, c],
-               me, other).wait_recv()
+    def s_wait(d, k, slot, c):
+        done(gin.at[slot, :, part_of(c)], l_recv.at[d, k, c]).wait_recv()
 
     def t_copy(k, slot):
-        return remote(send_s, table.at[slot], t_send.at[k], t_recv.at[slot], line(k) * plane + w, col)
+        return remote(send_s, table.at[slot], t_send, t_recv, line(k) * plane + w, col)
 
     feat_copy.wait()
     pl.semaphore_wait(barrier, top + plane)
@@ -173,7 +178,7 @@
 
         lax.fori_loop(0, plane, fill, 0, unroll=4)
         recvb[s, w] = sendb[s, w]
-        if i < top:
+        if i == 0:
             back_send(s)
 
     def link(lasts, key, index):
@@ -207,7 +212,7 @@
             zm = z + low_side * (top - 2 * z)
             rel = g - 1 + jnp.where(g <= zm, 0, 1)
             s = rel + low_side * (top - 2 * rel)
-        peers(lambda peer: pf_copy(s, peer, peer, whole).wait_recv())
+        from_peers(recvf, pf_recv, s)
 
         def step(k, lasts):
             slot = lax.rem(w + k, plane)
@@ -255,11 +260,13 @@
                 def _():
                     spread(lines[(d * top + k) * CH + c], feat_of(k, d), part_of(c))
 
+    is_end = (z == 0) | (z == top)
+
     def grads(k):
         for d in range(2):
             @pl.when(below[d] <= k)
             def _():
-                peers(lambda peer: pb_copy(sum_of(k, d), peer, peer).wait_recv())
+                from_peers(recvb, pb_recv, sum_of(k, d))
 
         step = tall // 2
         for c in range(CH):
@@ -270,7 +277,7 @@
 
                     @pl.when(below[d] > 0)
                     def _():
-                        s_wait(s, c)
+                        s_wait(d, k, s, c)
 
                     def some(i, carry):
                         at = pl.ds(pl.multiple_of(c * tall + i * step, step), step)
@@ -280,12 +287,12 @@
                         return carry
 
                     lax.fori_loop(0, tall // step, some, 0)
-                    s_copy(d, s, c).start()
-
-    for k in range(1, Q):
-        t_copy(k, line(k)).wait_recv()
+                    s_copy(d, k, s, c).start()
+
+    done(table.at[pl.ds(0, top)], t_recv).wait_recv()
 
     feats(0)
+    back_send(near)
     grads(0)
     lasts = lax.fori_loop(0, slots, own_back, (jnp.int32(0),) * half, unroll=unroll)
     for j in range(half):
@@ -294,11 +301,17 @@
     grads(1)
     lasts = lax.fori_loop(0, slots, own_fwd, (jnp.int32(0),) * blocks, unroll=unroll)
     lasts = slot_group(0, lasts)
+    lasts = slot_group(1, lasts)
     feats(2)
+    back_send(pair)
     back_send(z)
-    grads(2)
-    for g in range(1, Q):
-        lasts = slot_group(g, lasts)
+    lasts = slot_group(2, lasts)
+
+    @pl.when(jnp.logical_not(is_end))
+    def _():
+        grads(2)
+
+    lasts = slot_group(3, lasts)
 
     for r in range(blocks):
         part[r * blk:(r + 1) * blk, :] = buf[lasts[r]].astype(BF16)
@@ -316,11 +329,8 @@
     is_owner = (me >= first) & (me < first + doms)
 
     def r_copy(o):
-        return remote(wchunk.at[o], wpart.at[flat], r_send.at[o], r_recv.at[flat],
+        return remote(wchunk.at[o], wpart.at[flat], r_send, r_recv,
                       first + lax.div(o, 2), lax.rem(o, 2))
-
-    def r_in(f):
-        return remote(wchunk.at[0], wpart.at[f], r_send.at[0], r_recv.at[f], me, other)
 
     def others(limit, start, skip, body):
         def step(k, carry):
@@ -334,36 +344,37 @@
         lax.fori_loop(0, limit, step, 0)
 
     others(held, lax.rem(flat, held), mine, lambda o: r_copy(o).start())
+
+    @pl.when(is_end)
+    def _():
+        grads(2)
 
     p_copy.wait()
     for j in range(half):
         whose = buf[jnp.where(col == 0, lasts[j], lasts[half + j])]
         hid[pl.ds(j * blk, blk), :] = (whose + precv[j]).astype(BF16)
     out[...] = jnp.dot(hid[...], weight[...], preferred_element_type=F32).astype(BF16)
-    out_copy = pltpu.make_async_copy(out, out_hbm, misc.at[8])
+    out_copy = pltpu.make_async_copy(out, out_hbm, misc.at[0])
     out_copy.start()
 
     def g_copy(f):
-        return remote(wall.at[mine], wall.at[mine], g_send.at[f], g_recv.at[mine], lax.div(f, 2), lax.rem(f, 2))
-
-    def g_in(o):
-        return remote(wall.at[o], wall.at[o], g_send.at[0], g_recv.at[o], me, other)
+        return remote(wall.at[mine], wall.at[mine], g_send, g_recv, lax.div(f, 2), lax.rem(f, 2))
 
     @pl.when(is_owner)
     def _():
         wpart[flat] = wchunk[mine]
-        others(2 * n, flat, flat, lambda f: r_in(f).wait_recv())
+        done(wpart.at[pl.ds(0, 2 * n - 1)], r_recv).wait_recv()
         total = lax.fori_loop(0, 2 * n, lambda f, acc: acc + wpart[f].astype(F32),
                               jnp.zeros(wpart.shape[1:], F32), unroll=4)
         wall[mine] = total.astype(BF16)
         others(2 * n, flat, flat, lambda f: g_copy(f).start())
 
-    peers(lambda peer: pb_copy(z, peer, peer).wait_recv())
+    from_peers(recvb, pb_recv, z)
     for c in range(CH):
         for d in range(2):
             @pl.when(below[d] > 0)
             def _():
-                s_wait(z if d == 0 else Q, c)
+                s_wait(d, top, z if d == 0 else Q, c)
 
     step = 16
 
@@ -377,38 +388,37 @@
         return carry
 
     lax.fori_loop(0, blk // step, final, 0)
-    fgrad_copy = pltpu.make_async_copy(fgrad, fgrad_hbm, misc.at[9])
+    fgrad_copy = pltpu.make_async_copy(fgrad, fgrad_hbm, misc.at[1])
     fgrad_copy.start()
 
-    for k in range(1, Q):
-        t_copy(k, z).wait_send()
-    for s in range(Q):
-        def sent(peer, s=s):
-            pf_copy(s, peer, w, whole).wait_send()
-            pb_copy(s, peer, w).wait_send()
-
-        peers(sent)
-    for c in range(CH):
-        for d in range(2):
-            for k in range(Q - 1):
-                @pl.when((k <= below[d]) & (below[d] < top))
-                def _():
-                    lf_copy(d, k, c).wait_send()
-
-                @pl.when(below[d] <= k)
-                def _():
-                    s_copy(d, sum_of(k, d), c).wait_send()
+    done(table.at[pl.ds(0, top)], t_send).wait_send()
+    done(sendf.at[:, pl.ds(0, plane - 1)], pf_send).wait_send()
+    done(sendb.at[:, pl.ds(0, plane - 1)], pb_send).wait_send()
+    for d in range(2):
+        for k in range(top):
+            @pl.when(below[d] == k)
+            def _():
+                done(gin.at[pl.ds(0, k + 1)], lf_send.at[d]).wait_send()
+                done(gin.at[pl.ds(0, top - k)], s_send.at[d]).wait_send()
     c_copy.wait_send()
-    others(held, 0, mine, lambda o: r_copy(o).wait_send())
-
-    others(held, 0, mine, lambda o: g_in(o).wait_recv())
-    wgrad[...] = wall[...].astype(F32).reshape(wgrad.shape)
-    wgrad_copy = pltpu.make_async_copy(wgrad, wgrad_hbm, misc.at[10])
-    wgrad_copy.start()
 
     @pl.when(is_owner)
     def _():
-        others(2 * n, 0, flat, lambda f: g_copy(f).wait_send())
+        done(wchunk.at[pl.ds(0, held - 1)], r_send).wait_send()
+        done(wchunk.at[pl.ds(0, held - 1)], g_recv).wait_recv()
+
+    @pl.when(jnp.logical_not(is_owner))
+    def _():
+        done(wchunk, r_send).wait_send()
+        done(wchunk, g_recv).wait_recv()
+
+    wgrad[...] = wall[...].astype(F32).reshape(wgrad.shape)
+    wgrad_copy = pltpu.make_async_copy(wgrad, wgrad_hbm, misc.at[2])
+    wgrad_copy.start()
+
+    @pl.when(is_owner)
+    def _():
+        done(wpart.at[pl.ds(0, 2 * n - 1)], g_send).wait_send()
 
     out_copy.wait()
     fgrad_copy.wait()
@@ -492,11 +502,9 @@
             pltpu.SMEM((n,), jnp.int32),
             pltpu.SMEM((Q, n), jnp.int32),
         ] + [pltpu.VMEM((half, blk // CH, width), bf)] * (2 * (Q - 1) * CH) + [
-            sems((Q,)), sems((Q,)),
-            sems((2, Q - 1, CH)), sems((2, Q - 1, CH)),
-            sems((Q, CH)), sems((Q + 1, CH)),
-        ] + [sems((Q, plane))] * 4 + [
-            sems((2 * doms,)), sems((2 * n,)), sems((2 * n,)), sems((2 * doms,)), sems((11,)),
+            sems(()), sems(()), sems((2,)), sems((2,)), sems((2, Q, CH)),
+            sems(()), sems((Q,)), sems(()), sems((Q,)),
+            sems(()), sems(()), sems(()), sems(()), sems((8,)),
         ],
         compiler_params=pltpu.CompilerParams(
             collective_id=0, has_side_effects=True, vmem_limit_bytes=67000000),

time: 47.5 us -> 47.6 us (level)
  no operation moved by 1% of the time
where the time goes in v3:
time: 47.6 us; the launch traced here: 47.4 us
  Pallas kernels  46.1 us (97%)
  between operations  1.29 us (3%)
    pallas_call x1, Pallas kernels, local(): pl.pallas_call(functools.partial(kernel, scale, owners), out_shape=(jax.S...  44.2 us
    pallas_call x1, Pallas kernels, finish(): pl.pallas_call(place, out_shape=tuple((jax.ShapeDtypeStruct(a.shape, a.dt...  1.88 us

profile of v3, /device:TPU:0, one launch (start us, length us, event | category | flops | bytes accessed | tf_op | source)
XLA Modules:
  0.0 47.4 jit_solution(16806772898540622820)
XLA Ops:
  1.3 44.2 %shard_map.103 = (bf16[512,256]{1,0:T(8,128)(2,1)}, bf16[4,128,256]{2,1,0:T(8,128)(2,1)}, f32[256,256]{1,0:T(8,128)}) custom-call(s32[40]{0:T(128)} %rows_s.1, s32[40]{0:T(128)} %cols_s.1, s32[1]{0:T(128)S(6)} %copy.11.count_s, s32[16]{0:T(128)} %bitcast.5, bf16[4,128,256]{2,1,0:T(8,128)(2,1)} %bitcast.3, bf16[256,256]{1,0:T(8,128)(2,1)} %weight_hbm.1, ...), custom_call_target="tpu_custom_call" | custom-call | tf_op jit(solution)/shard_map/pallas_call | solution.py:470
  45.5 1.9 %shard_map.104 = (bf16[512,256]{1,0:T(8,128)(2,1)}, bf16[512,256]{1,0:T(8,128)(2,1)}, f32[256,256]{1,0:T(8,128)}) custom-call(bf16[512,256]{1,0:T(8,128)(2,1)} %get-tuple-element.6.refs_0_, bf16[512,256]{1,0:T(8,128)(2,1)} %bitcast.4, f32[256,256]{1,0:T(8,128)} %get-tuple-element.8.refs_2_), custom_call_target="tpu_custom_call" | custom-call | tf_op jit(solution)/shard_map/pallas_call | solution.py:444

commit v4 on v3

--- a/solution.py
+++ b/solution.py
@@ -14,10 +14,11 @@
 CH = 4
 
 
-def kernel(scale, owners, rows_s, cols_s, count_s, send_s, feat_hbm, weight_hbm, cot_hbm, tiles_hbm,
-           out_hbm, fgrad_hbm, wgrad_hbm,
+def kernel(scale, owners, rows_hbm, cols_hbm, count_s, send_hbm, feat_hbm, weight_hbm, cot_hbm, tiles_hbm,
+           out, fgrad, wgrad,
            feat, weight, cot, tiles, sendf, recvf, sendb, recvb, gin, buf, base, gh, psend, precv, hid,
-           part, out, fgrad, wgrad, wchunk, wpart, wall, tos, table, *rest):
+           part, wterm, whalf, wpeer, wchunk, wpart, wall, tos, table,
+           rows_s, cols_s, send_s, *rest):
     lines = rest[:2 * (Q - 1) * CH]
     (t_send, t_recv, lf_send, s_send, l_recv, pf_send, pf_recv, pb_send, pb_recv,
      r_send, r_recv, g_send, g_recv, misc) = rest[2 * (Q - 1) * CH:]
@@ -34,7 +35,6 @@
     count = count_s[0]
     z, w = lax.div(me, plane), lax.rem(me, plane)
     below = (z, top - z)
-    flat = 2 * me + col
 
     def remote(src, dst, s_sem, r_sem, dom, core):
         return pltpu.make_async_remote_copy(
@@ -53,6 +53,10 @@
 
     feat_copy = pltpu.make_async_copy(feat_hbm, feat, misc.at[0])
     feat_copy.start()
+    smalls = [pltpu.make_async_copy(a, b, misc.at[12 + i]) for i, (a, b) in enumerate(
+        ((send_hbm, send_s), (rows_hbm, rows_s), (cols_hbm, cols_s)))]
+    for small in smalls:
+        small.start()
     barrier = pltpu.get_barrier_semaphore()
 
     def greet(dom, core):
@@ -74,6 +78,9 @@
     gin[...] = jnp.zeros(gin.shape, gin.dtype)
     buf[0] = jnp.zeros((blk, width), F32)
 
+    for small in smalls:
+        small.wait()
+
     def keep(i, carry):
         table[z, i] = send_s[i]
         return carry
@@ -260,8 +267,6 @@
                 def _():
                     spread(lines[(d * top + k) * CH + c], feat_of(k, d), part_of(c))
 
-    is_end = (z == 0) | (z == top)
-
     def grads(k):
         for d in range(2):
             @pl.when(below[d] <= k)
@@ -289,85 +294,93 @@
                     lax.fori_loop(0, tall // step, some, 0)
                     s_copy(d, k, s, c).start()
 
+    lasts = lax.fori_loop(0, slots, own_back, (jnp.int32(0),) * half, unroll=unroll)
+    for j in range(half):
+        base[j] = buf[lasts[j]]
     done(table.at[pl.ds(0, top)], t_recv).wait_recv()
 
+    is_end = (z == 0) | (z == top)
     feats(0)
     back_send(near)
     grads(0)
-    lasts = lax.fori_loop(0, slots, own_back, (jnp.int32(0),) * half, unroll=unroll)
-    for j in range(half):
-        base[j] = buf[lasts[j]]
     feats(1)
     grads(1)
-    lasts = lax.fori_loop(0, slots, own_fwd, (jnp.int32(0),) * blocks, unroll=unroll)
-    lasts = slot_group(0, lasts)
-    lasts = slot_group(1, lasts)
+
+    @pl.when(jnp.logical_not(is_end))
+    def _():
+        back_send(pair)
+        back_send(z)
+
+    lasts = slot_group(0, (jnp.int32(0),) * blocks)
     feats(2)
-    back_send(pair)
-    back_send(z)
-    lasts = slot_group(2, lasts)
-
-    @pl.when(jnp.logical_not(is_end))
-    def _():
-        grads(2)
-
-    lasts = slot_group(3, lasts)
+
+    @pl.when(is_end)
+    def _():
+        back_send(pair)
+
+    lasts = lax.fori_loop(0, slots, own_fwd, lasts, unroll=unroll)
+    for g in range(1, Q):
+        lasts = slot_group(g, lasts)
 
     for r in range(blocks):
         part[r * blk:(r + 1) * blk, :] = buf[lasts[r]].astype(BF16)
+    wterm[...] = lax.dot_general(part[...], cot[...], (((0,), (0,)), ((), ())),
+                                 preferred_element_type=F32) * jnp.float32(scale)
+    d_copy = remote(whalf, wpeer, misc.at[8], misc.at[9], me, other)
+
+    @pl.when(col == 0)
+    def _():
+        whalf[...] = wterm[...].astype(BF16)
+        d_copy.start()
+
+    first, doms = owners
+    mine = me - first
+    is_owner = (col == 1) & (me >= first) & (me < first + doms)
+
+    def others(limit, start, skip, body):
+        def step(k, carry):
+            at = lax.rem(start + k, limit)
+
+            @pl.when(at != skip)
+            def _():
+                body(at)
+            return carry
+
+        lax.fori_loop(0, limit, step, 0)
+
+    @pl.when(col == 1)
+    def _():
+        d_copy.wait_recv()
+        wchunk[...] = (wterm[...] + wpeer[...].astype(F32)).astype(BF16).reshape(wchunk.shape)
+        others(doms, lax.rem(me, doms), mine,
+               lambda i: remote(wchunk.at[i], wpart.at[me], r_send, r_recv, first + i, 1).start())
+
     for j in range(half):
         psend[j] = buf[jnp.where(col == 0, lasts[half + j], lasts[j])]
     p_copy = remote(psend, precv, misc.at[6], misc.at[7], me, other)
     p_copy.start()
-    term = lax.dot_general(part[...], cot[...], (((0,), (0,)), ((), ())),
-                           preferred_element_type=F32) * jnp.float32(scale)
-    wchunk[...] = term.astype(BF16).reshape(wchunk.shape)
-
-    first, doms = owners
-    held = 2 * doms
-    mine = flat - 2 * first
-    is_owner = (me >= first) & (me < first + doms)
-
-    def r_copy(o):
-        return remote(wchunk.at[o], wpart.at[flat], r_send, r_recv,
-                      first + lax.div(o, 2), lax.rem(o, 2))
-
-    def others(limit, start, skip, body):
-        def step(k, carry):
-            at = lax.rem(start + k, limit)
-
-            @pl.when(at != skip)
-            def _():
-                body(at)
-            return carry
-
-        lax.fori_loop(0, limit, step, 0)
-
-    others(held, lax.rem(flat, held), mine, lambda o: r_copy(o).start())
 
     @pl.when(is_end)
     def _():
-        grads(2)
+        back_send(z)
+
+    grads(2)
 
     p_copy.wait()
     for j in range(half):
         whose = buf[jnp.where(col == 0, lasts[j], lasts[half + j])]
         hid[pl.ds(j * blk, blk), :] = (whose + precv[j]).astype(BF16)
     out[...] = jnp.dot(hid[...], weight[...], preferred_element_type=F32).astype(BF16)
-    out_copy = pltpu.make_async_copy(out, out_hbm, misc.at[0])
-    out_copy.start()
-
-    def g_copy(f):
-        return remote(wall.at[mine], wall.at[mine], g_send, g_recv, lax.div(f, 2), lax.rem(f, 2))
 
     @pl.when(is_owner)
     def _():
-        wpart[flat] = wchunk[mine]
-        done(wpart.at[pl.ds(0, 2 * n - 1)], r_recv).wait_recv()
-        total = lax.fori_loop(0, 2 * n, lambda f, acc: acc + wpart[f].astype(F32),
+        wpart[me] = wchunk[mine]
+        done(wpart.at[pl.ds(0, n - 1)], r_recv).wait_recv()
+        total = lax.fori_loop(0, n, lambda f, acc: acc + wpart[f].astype(F32),
                               jnp.zeros(wpart.shape[1:], F32), unroll=4)
         wall[mine] = total.astype(BF16)
-        others(2 * n, flat, flat, lambda f: g_copy(f).start())
+        others(n, me, me,
+               lambda f: remote(wall.at[mine], wall.at[mine], g_send, g_recv, f, 1).start())
 
     from_peers(recvb, pb_recv, z)
     for c in range(CH):
@@ -388,8 +401,6 @@
         return carry
 
     lax.fori_loop(0, blk // step, final, 0)
-    fgrad_copy = pltpu.make_async_copy(fgrad, fgrad_hbm, misc.at[1])
-    fgrad_copy.start()
 
     done(table.at[pl.ds(0, top)], t_send).wait_send()
     done(sendf.at[:, pl.ds(0, plane - 1)], pf_send).wait_send()
@@ -402,53 +413,64 @@
                 done(gin.at[pl.ds(0, top - k)], s_send.at[d]).wait_send()
     c_copy.wait_send()
 
+    h_copy = remote(wall, wall, misc.at[10], misc.at[11], me, other)
+
     @pl.when(is_owner)
     def _():
-        done(wchunk.at[pl.ds(0, held - 1)], r_send).wait_send()
-        done(wchunk.at[pl.ds(0, held - 1)], g_recv).wait_recv()
-
-    @pl.when(jnp.logical_not(is_owner))
+        done(wchunk.at[pl.ds(0, doms - 1)], g_recv).wait_recv()
+
+    @pl.when((col == 1) & jnp.logical_not(is_owner))
+    def _():
+        done(wchunk, g_recv).wait_recv()
+
+    @pl.when(col == 1)
+    def _():
+        h_copy.start()
+
+    @pl.when(col == 0)
+    def _():
+        h_copy.wait_recv()
+        d_copy.wait_send()
+
+    wgrad[...] = wall[...].astype(F32).reshape(wgrad.shape)
+
+    @pl.when(is_owner)
+    def _():
+        done(wchunk.at[pl.ds(0, doms - 1)], r_send).wait_send()
+        done(wpart.at[pl.ds(0, n - 1)], g_send).wait_send()
+
+    @pl.when((col == 1) & jnp.logical_not(is_owner))
     def _():
         done(wchunk, r_send).wait_send()
-        done(wchunk, g_recv).wait_recv()
-
-    wgrad[...] = wall[...].astype(F32).reshape(wgrad.shape)
-    wgrad_copy = pltpu.make_async_copy(wgrad, wgrad_hbm, misc.at[2])
-    wgrad_copy.start()
-
-    @pl.when(is_owner)
-    def _():
-        done(wpart.at[pl.ds(0, 2 * n - 1)], g_send).wait_send()
-
-    out_copy.wait()
-    fgrad_copy.wait()
-    wgrad_copy.wait()
+
+    @pl.when(col == 1)
+    def _():
+        h_copy.wait_send()
 
 
 def place(*refs):
-    count = (len(refs) - 1) // 3
-    sources, targets, held, sem = refs[:count], refs[count:2 * count], refs[2 * count:-1], refs[-1]
-    reads = [pltpu.make_async_copy(a, h, sem.at[i]) for i, (a, h) in enumerate(zip(sources, held))]
-    writes = [pltpu.make_async_copy(h, b, sem.at[count + i]) for i, (h, b) in enumerate(zip(held, targets))]
-    for read in reads:
-        read.start()
-    for read, write in zip(reads, writes):
-        read.wait()
+    count = len(refs) // 2
+    sem = refs[-1]
+    writes = [pltpu.make_async_copy(a, b, sem.at[i]) for i, (a, b) in enumerate(zip(refs[:count], refs[count:-1]))]
+    for write in writes:
         write.start()
     for write in writes:
         write.wait()
 
 
 def finish(*arrays):
-    hbm = pl.BlockSpec(memory_space=pl.ANY)
     return pl.pallas_call(
         place,
         out_shape=tuple(jax.ShapeDtypeStruct(a.shape, a.dtype) for a in arrays),
-        in_specs=[hbm] * len(arrays),
-        out_specs=(hbm,) * len(arrays),
-        scratch_shapes=[pltpu.VMEM(a.shape, a.dtype) for a in arrays]
-        + [pltpu.SemaphoreType.DMA((2 * len(arrays),))],
+        in_specs=[pl.BlockSpec(memory_space=pltpu.VMEM)] * len(arrays),
+        out_specs=(pl.BlockSpec(memory_space=pltpu.HBM),) * len(arrays),
+        scratch_shapes=[pltpu.SemaphoreType.DMA((len(arrays),))],
+        compiler_params=pltpu.CompilerParams(vmem_limit_bytes=4000000),
     )(*arrays)
+
+
+def in_hbm(array):
+    return pltpu.with_memory_space_constraint(array, pltpu.HBM)
 
 
 def local(features, weight, cotangent, tile_values, tile_rows, tile_cols, tile_count, send_blocks):
@@ -463,8 +485,9 @@
     bf = jnp.bfloat16
     doms = min(n // 2, width // 16)
     owners = (n // 4, doms)
-    chunk = width // (2 * doms)
-    hbm = pl.BlockSpec(memory_space=pl.ANY)
+    chunk = width // doms
+    hbm = pl.BlockSpec(memory_space=pltpu.HBM)
+    vmem = pl.BlockSpec(memory_space=pltpu.VMEM)
     smem = pl.BlockSpec(memory_space=pltpu.SMEM)
     sems = pltpu.SemaphoreType.DMA
     out, fgrad, wgrad = pl.pallas_call(
@@ -474,8 +497,8 @@
             jax.ShapeDtypeStruct((half, blk, width), bf),
             jax.ShapeDtypeStruct((width, width_out), F32),
         ),
-        in_specs=[smem] * 4 + [hbm] * 4,
-        out_specs=(hbm, hbm, hbm),
+        in_specs=[hbm, hbm, smem] + [hbm] * 5,
+        out_specs=(vmem, vmem, vmem),
         scratch_shapes=[
             pltpu.VMEM((half, blk, width), bf),
             pltpu.VMEM((width, width_out), bf),
@@ -493,23 +516,26 @@
             pltpu.VMEM((half, blk, width), F32),
             pltpu.VMEM((rows, width), bf),
             pltpu.VMEM((2 * rows, width), bf),
-            pltpu.VMEM((rows, width_out), bf),
-            pltpu.VMEM((half, blk, width), bf),
             pltpu.VMEM((width, width_out), F32),
-            pltpu.VMEM((2 * doms, chunk, width_out), bf),
-            pltpu.VMEM((2 * n, chunk, width_out), bf),
-            pltpu.VMEM((2 * doms, chunk, width_out), bf),
+            pltpu.VMEM((width, width_out), bf),
+            pltpu.VMEM((width, width_out), bf),
+            pltpu.VMEM((doms, chunk, width_out), bf),
+            pltpu.VMEM((n, chunk, width_out), bf),
+            pltpu.VMEM((doms, chunk, width_out), bf),
             pltpu.SMEM((n,), jnp.int32),
             pltpu.SMEM((Q, n), jnp.int32),
+            pltpu.SMEM((slots,), jnp.int32),
+            pltpu.SMEM((slots,), jnp.int32),
+            pltpu.SMEM((n,), jnp.int32),
         ] + [pltpu.VMEM((half, blk // CH, width), bf)] * (2 * (Q - 1) * CH) + [
             sems(()), sems(()), sems((2,)), sems((2,)), sems((2, Q, CH)),
             sems(()), sems((Q,)), sems(()), sems((Q,)),
-            sems(()), sems(()), sems(()), sems(()), sems((8,)),
+            sems(()), sems(()), sems(()), sems(()), sems((15,)),
         ],
         compiler_params=pltpu.CompilerParams(
-            collective_id=0, has_side_effects=True, vmem_limit_bytes=67000000),
-    )(tile_rows, tile_cols, tile_count, send_blocks.reshape(n),
-      features.reshape(half, blk, width), weight, cotangent, tile_values)
+            collective_id=0, has_side_effects=True, vmem_limit_bytes=min(67000000, 20000000 + 12 * n * blk * width)),
+    )(in_hbm(tile_rows), in_hbm(tile_cols), tile_count, in_hbm(send_blocks.reshape(n)),
+      in_hbm(features.reshape(half, blk, width)), in_hbm(weight), in_hbm(cotangent), in_hbm(tile_values))
     return finish(out, fgrad.reshape(rows, width), wgrad)
 
 

time: 47.6 us -> 42.2 us (0.89)
  Pallas kernels: 46.1 us -> 40.8 us
    pallas_call x1, Pallas kernels: 44.2 us -> 39.9 us  [local(): pl.pallas_call(functools.partial(kernel, scale, owners), out_shape=(jax.S...]
    pallas_call x1, Pallas kernels: 1.88 us -> 0.9 us  [finish(): pl.pallas_call(place, out_shape=tuple((jax.ShapeDtypeStruct(a.shape, a.dt...]
where the time goes in v4:
time: 42.2 us; the launch traced here: 42.1 us
  Pallas kernels  40.8 us (97%)
  between operations  1.29 us (3%)
    pallas_call x1, Pallas kernels, local(): pl.pallas_call(functools.partial(kernel, scale, owners), out_shape=(jax.S...  39.9 us
    pallas_call x1, Pallas kernels, finish(): pl.pallas_call(place, out_shape=tuple((jax.ShapeDtypeStruct(a.shape, a.dt...  0.9 us

profile of v4, /device:TPU:0, one launch (start us, length us, event | category | flops | bytes accessed | tf_op | source)
XLA Modules:
  0.0 42.1 jit_solution(1635074814902863411)
XLA Ops:
  1.3 39.9 %shard_map.103 = (bf16[512,256]{1,0:T(8,128)(2,1)S(1)}, bf16[4,128,256]{2,1,0:T(8,128)(2,1)S(1)}, f32[256,256]{1,0:T(8,128)S(1)}) custom-call(s32[40]{0:T(128)} %rows_hbm.1, s32[40]{0:T(128)} %cols_hbm.1, s32[1]{0:T(128)S(6)} %copy.11.count_s, s32[16]{0:T(128)} %bitcast.5, bf16[4,128,256]{2,1,0:T(8,128)(2,1)} %bitcast.4, bf16[256,256]{1,0:T(8,128)(2,1)} %weight_hbm.1, ...), custom_call_target="tpu_custom_call" | custom-call | tf_op jit(solution)/shard_map/pallas_call | solution.py:493
  41.2 0.9 %shard_map.104 = (bf16[512,256]{1,0:T(8,128)(2,1)}, bf16[512,256]{1,0:T(8,128)(2,1)}, f32[256,256]{1,0:T(8,128)}) custom-call(bf16[512,256]{1,0:T(8,128)(2,1)S(1)} %get-tuple-element.6.refs_0_, bf16[512,256]{1,0:T(8,128)(2,1)S(1)} %bitcast.3, f32[256,256]{1,0:T(8,128)S(1)} %get-tuple-element.8.refs_2_), custom_call_target="tpu_custom_call" | custom-call | tf_op jit(solution)/shard_map/pallas_call | solution.py:462

commit v5 on v4

--- a/solution.py
+++ b/solution.py
@@ -16,12 +16,13 @@
 
 def kernel(scale, owners, rows_hbm, cols_hbm, count_s, send_hbm, feat_hbm, weight_hbm, cot_hbm, tiles_hbm,
            out, fgrad, wgrad,
-           feat, weight, cot, tiles, sendf, recvf, sendb, recvb, gin, buf, base, gh, psend, precv, hid,
-           part, wterm, whalf, wpeer, wchunk, wpart, wall, tos, table,
+           feat, weight, cot, tiles, sendf, recvf, sendb, recvb, gin, buf, base, gh, psend, precv,
+           sendx, wchunk, wpart, wall, tos, table,
            rows_s, cols_s, send_s, *rest):
-    lines = rest[:2 * (Q - 1) * CH]
+    hops = Q - 2
+    lines = rest[:2 * hops * CH]
     (t_send, t_recv, lf_send, s_send, l_recv, pf_send, pf_recv, pb_send, pb_recv,
-     r_send, r_recv, g_send, g_recv, misc) = rest[2 * (Q - 1) * CH:]
+     x_send, r_send, r_recv, g_send, g_recv, misc) = rest[2 * hops * CH:]
     slots = tiles.shape[0]
     half, blk, width = feat.shape
     plane = recvf.shape[1]
@@ -35,6 +36,7 @@
     count = count_s[0]
     z, w = lax.div(me, plane), lax.rem(me, plane)
     below = (z, top - z)
+    is_end = (z == 0) | (z == top)
 
     def remote(src, dst, s_sem, r_sem, dom, core):
         return pltpu.make_async_remote_copy(
@@ -116,8 +118,8 @@
 
     def lf_copy(d, k, c):
         nxt = z + 1 if d == 0 else z - 1
-        src = feat.at[:, part_of(c)] if k == 0 else lines[(d * top + k - 1) * CH + c]
-        return remote(src, lines[(d * top + k) * CH + c], lf_send.at[d], l_recv.at[d, k, c],
+        src = feat.at[:, part_of(c)] if k == 0 else lines[(d * hops + k - 1) * CH + c]
+        return remote(src, lines[(d * hops + k) * CH + c], lf_send.at[d], l_recv.at[d, k, c],
                       nxt * plane + w, col)
 
     def s_copy(d, k, s, c):
@@ -219,7 +221,17 @@
             zm = z + low_side * (top - 2 * z)
             rel = g - 1 + jnp.where(g <= zm, 0, 1)
             s = rel + low_side * (top - 2 * rel)
-        from_peers(recvf, pf_recv, s)
+        if g < top:
+            from_peers(recvf, pf_recv, s)
+        else:
+            @pl.when(is_end)
+            def _():
+                done(recvf.at[s], pf_recv.at[s]).wait_recv()
+
+            @pl.when(jnp.logical_not(is_end))
+            def _():
+                from_peers(recvf, pf_recv, s)
+
 
         def step(k, lasts):
             slot = lax.rem(w + k, plane)
@@ -250,6 +262,22 @@
         rel = below[d] - 1 - k
         return rel if d == 0 else top - rel
 
+    def reach(d, source, s, at):
+        nxt = (z + 1 if d == 0 else z - 1) * plane
+
+        def one(k, carry):
+            peer = lax.rem(w + k, plane)
+            sendx[peer, at, :] = source[table[s, nxt + peer]]
+            return carry
+
+        def go(k, carry):
+            peer = lax.rem(w + k, plane)
+            remote(sendx.at[peer, at], recvf.at[s, w, at], x_send, pf_recv.at[s], nxt + peer, col).start()
+            return carry
+
+        lax.fori_loop(0, plane, one, 0)
+        lax.fori_loop(0, plane, go, 0)
+
     def feats(k):
         for c in range(CH):
             for d in range(2):
@@ -257,15 +285,17 @@
                 def _():
                     lf_copy(d, k, c).wait_recv()
 
-                    if k + 1 < top:
-                        @pl.when(below[d] < top)
-                        def _():
+                    @pl.when(below[d] < top)
+                    def _():
+                        if k + 1 < hops:
                             lf_copy(d, k + 1, c).start()
+                        else:
+                            reach(d, lines[(d * hops + k) * CH + c], feat_of(k, d), part_of(c))
 
             for d in range(2):
                 @pl.when(k < below[d])
                 def _():
-                    spread(lines[(d * top + k) * CH + c], feat_of(k, d), part_of(c))
+                    spread(lines[(d * hops + k) * CH + c], feat_of(k, d), part_of(c))
 
     def grads(k):
         for d in range(2):
@@ -299,39 +329,28 @@
         base[j] = buf[lasts[j]]
     done(table.at[pl.ds(0, top)], t_recv).wait_recv()
 
-    is_end = (z == 0) | (z == top)
     feats(0)
     back_send(near)
     grads(0)
     feats(1)
     grads(1)
 
+    back_send(pair)
+
     @pl.when(jnp.logical_not(is_end))
     def _():
-        back_send(pair)
         back_send(z)
 
     lasts = slot_group(0, (jnp.int32(0),) * blocks)
-    feats(2)
-
-    @pl.when(is_end)
-    def _():
-        back_send(pair)
-
     lasts = lax.fori_loop(0, slots, own_fwd, lasts, unroll=unroll)
     for g in range(1, Q):
         lasts = slot_group(g, lasts)
 
     for r in range(blocks):
-        part[r * blk:(r + 1) * blk, :] = buf[lasts[r]].astype(BF16)
-    wterm[...] = lax.dot_general(part[...], cot[...], (((0,), (0,)), ((), ())),
-                                 preferred_element_type=F32) * jnp.float32(scale)
-    d_copy = remote(whalf, wpeer, misc.at[8], misc.at[9], me, other)
-
-    @pl.when(col == 0)
-    def _():
-        whalf[...] = wterm[...].astype(BF16)
-        d_copy.start()
+        gh[r] = buf[lasts[r]].astype(BF16)
+    term = lax.dot_general(gh[...].reshape(cot.shape), cot[...], (((0,), (0,)), ((), ())),
+                           preferred_element_type=F32) * jnp.float32(scale)
+    wchunk[...] = term.astype(BF16).reshape(wchunk.shape)
 
     first, doms = owners
     mine = me - first
@@ -348,12 +367,10 @@
 
         lax.fori_loop(0, limit, step, 0)
 
-    @pl.when(col == 1)
-    def _():
-        d_copy.wait_recv()
-        wchunk[...] = (wterm[...] + wpeer[...].astype(F32)).astype(BF16).reshape(wchunk.shape)
-        others(doms, lax.rem(me, doms), mine,
-               lambda i: remote(wchunk.at[i], wpart.at[me], r_send, r_recv, first + i, 1).start())
+    flat = 2 * me + col
+    keep_own = jnp.where(is_owner, mine, doms)
+    others(doms, lax.rem(me, doms), keep_own,
+           lambda i: remote(wchunk.at[i], wpart.at[flat], r_send, r_recv, first + i, 1).start())
 
     for j in range(half):
         psend[j] = buf[jnp.where(col == 0, lasts[half + j], lasts[j])]
@@ -369,14 +386,14 @@
     p_copy.wait()
     for j in range(half):
         whose = buf[jnp.where(col == 0, lasts[j], lasts[half + j])]
-        hid[pl.ds(j * blk, blk), :] = (whose + precv[j]).astype(BF16)
-    out[...] = jnp.dot(hid[...], weight[...], preferred_element_type=F32).astype(BF16)
+        hidden = (whose + precv[j]).astype(BF16)
+        out[pl.ds(j * blk, blk), :] = jnp.dot(hidden, weight[...], preferred_element_type=F32).astype(BF16)
 
     @pl.when(is_owner)
     def _():
-        wpart[me] = wchunk[mine]
-        done(wpart.at[pl.ds(0, n - 1)], r_recv).wait_recv()
-        total = lax.fori_loop(0, n, lambda f, acc: acc + wpart[f].astype(F32),
+        wpart[flat] = wchunk[mine]
+        done(wpart.at[pl.ds(0, 2 * n - 1)], r_recv).wait_recv()
+        total = lax.fori_loop(0, 2 * n, lambda f, acc: acc + wpart[f].astype(F32),
                               jnp.zeros(wpart.shape[1:], F32), unroll=4)
         wall[mine] = total.astype(BF16)
         others(n, me, me,
@@ -403,13 +420,22 @@
     lax.fori_loop(0, blk // step, final, 0)
 
     done(table.at[pl.ds(0, top)], t_send).wait_send()
-    done(sendf.at[:, pl.ds(0, plane - 1)], pf_send).wait_send()
+
+    @pl.when(is_end)
+    def _():
+        done(sendf.at[pl.ds(0, top), pl.ds(0, plane - 1)], pf_send).wait_send()
+
+    @pl.when(jnp.logical_not(is_end))
+    def _():
+        done(sendf.at[:, pl.ds(0, plane - 1)], pf_send).wait_send()
+        done(sendx, x_send).wait_send()
+
     done(sendb.at[:, pl.ds(0, plane - 1)], pb_send).wait_send()
     for d in range(2):
         for k in range(top):
             @pl.when(below[d] == k)
             def _():
-                done(gin.at[pl.ds(0, k + 1)], lf_send.at[d]).wait_send()
+                done(gin.at[pl.ds(0, min(k + 1, hops))], lf_send.at[d]).wait_send()
                 done(gin.at[pl.ds(0, top - k)], s_send.at[d]).wait_send()
     c_copy.wait_send()
 
@@ -430,7 +456,6 @@
     @pl.when(col == 0)
     def _():
         h_copy.wait_recv()
-        d_copy.wait_send()
 
     wgrad[...] = wall[...].astype(F32).reshape(wgrad.shape)
 
@@ -439,7 +464,7 @@
         done(wchunk.at[pl.ds(0, doms - 1)], r_send).wait_send()
         done(wpart.at[pl.ds(0, n - 1)], g_send).wait_send()
 
-    @pl.when((col == 1) & jnp.logical_not(is_owner))
+    @pl.when(jnp.logical_not(is_owner))
     def _():
         done(wchunk, r_send).wait_send()
 
@@ -483,7 +508,7 @@
     nodes = rows * lax.axis_size("col") * lax.axis_size("dom")
     scale = 1.0 / nodes**0.5
     bf = jnp.bfloat16
-    doms = min(n // 2, width // 16)
+    doms = min(n // 2, width // 8)
     owners = (n // 4, doms)
     chunk = width // doms
     hbm = pl.BlockSpec(memory_space=pltpu.HBM)
@@ -514,23 +539,19 @@
             pltpu.VMEM((2 * half, blk, width), bf),
             pltpu.VMEM((half, blk, width), F32),
             pltpu.VMEM((half, blk, width), F32),
-            pltpu.VMEM((rows, width), bf),
-            pltpu.VMEM((2 * rows, width), bf),
-            pltpu.VMEM((width, width_out), F32),
-            pltpu.VMEM((width, width_out), bf),
-            pltpu.VMEM((width, width_out), bf),
+            pltpu.VMEM((plane, blk, width), bf),
             pltpu.VMEM((doms, chunk, width_out), bf),
-            pltpu.VMEM((n, chunk, width_out), bf),
+            pltpu.VMEM((2 * n, chunk, width_out), bf),
             pltpu.VMEM((doms, chunk, width_out), bf),
             pltpu.SMEM((n,), jnp.int32),
             pltpu.SMEM((Q, n), jnp.int32),
             pltpu.SMEM((slots,), jnp.int32),
             pltpu.SMEM((slots,), jnp.int32),
             pltpu.SMEM((n,), jnp.int32),
-        ] + [pltpu.VMEM((half, blk // CH, width), bf)] * (2 * (Q - 1) * CH) + [
+        ] + [pltpu.VMEM((half, blk // CH, width), bf)] * (2 * (Q - 2) * CH) + [
             sems(()), sems(()), sems((2,)), sems((2,)), sems((2, Q, CH)),
             sems(()), sems((Q,)), sems(()), sems((Q,)),
-            sems(()), sems(()), sems(()), sems(()), sems((15,)),
+            sems(()), sems(()), sems(()), sems(()), sems(()), sems((15,)),
         ],
         compiler_params=pltpu.CompilerParams(
             collective_id=0, has_side_effects=True, vmem_limit_bytes=min(67000000, 20000000 + 12 * n * blk * width)),

time: 42.2 us -> 40.6 us (0.962)
  Pallas kernels: 40.8 us -> 39.1 us
    pallas_call x1, Pallas kernels: 39.9 us -> 38.2 us  [local(): pl.pallas_call(functools.partial(kernel, scale, owners), out_shape=(jax.S...]
where the time goes in v5:
time: 40.6 us; the launch traced here: 40.4 us
  Pallas kernels  39.1 us (96%)
  between operations  1.29 us (3%)
    pallas_call x1, Pallas kernels, local(): pl.pallas_call(functools.partial(kernel, scale, owners), out_shape=(jax.S...  38.2 us
    pallas_call x1, Pallas kernels, finish(): pl.pallas_call(place, out_shape=tuple((jax.ShapeDtypeStruct(a.shape, a.dt...  0.9 us

profile of v5, /device:TPU:0, one launch (start us, length us, event | category | flops | bytes accessed | tf_op | source)
XLA Modules:
  0.0 40.4 jit_solution(18073521454335121218)
XLA Ops:
  1.3 38.2 %shard_map.103 = (bf16[512,256]{1,0:T(8,128)(2,1)S(1)}, bf16[4,128,256]{2,1,0:T(8,128)(2,1)S(1)}, f32[256,256]{1,0:T(8,128)S(1)}) custom-call(s32[40]{0:T(128)} %rows_hbm.1, s32[40]{0:T(128)} %cols_hbm.1, s32[1]{0:T(128)S(6)} %copy.11.count_s, s32[16]{0:T(128)} %bitcast.5, bf16[4,128,256]{2,1,0:T(8,128)(2,1)} %bitcast.4, bf16[256,256]{1,0:T(8,128)(2,1)} %weight_hbm.1, ...), custom_call_target="tpu_custom_call" | custom-call | tf_op jit(solution)/shard_map/pallas_call | solution.py:518
  39.5 0.9 %shard_map.104 = (bf16[512,256]{1,0:T(8,128)(2,1)}, bf16[512,256]{1,0:T(8,128)(2,1)}, f32[256,256]{1,0:T(8,128)}) custom-call(bf16[512,256]{1,0:T(8,128)(2,1)S(1)} %get-tuple-element.6.refs_0_, bf16[512,256]{1,0:T(8,128)(2,1)S(1)} %bitcast.3, f32[256,256]{1,0:T(8,128)S(1)} %get-tuple-element.8.refs_2_), custom_call_target="tpu_custom_call" | custom-call | tf_op jit(solution)/shard_map/pallas_call | solution.py:487

commit v6 on v5

--- a/solution.py
+++ b/solution.py
@@ -11,7 +11,7 @@
 F32 = jnp.float32
 BF16 = jnp.bfloat16
 Q = 4
-CH = 4
+CH = 2
 
 
 def kernel(scale, owners, rows_hbm, cols_hbm, count_s, send_hbm, feat_hbm, weight_hbm, cot_hbm, tiles_hbm,

time: 40.6 us -> 39.9 us (0.983)
  Pallas kernels: 39.1 us -> 38.5 us
    pallas_call x1, Pallas kernels: 38.2 us -> 37.6 us  [local(): pl.pallas_call(functools.partial(kernel, scale, owners), out_shape=(jax.S...]
where the time goes in v6:
time: 39.9 us; the launch traced here: 39.8 us
  Pallas kernels  38.5 us (96%)
  between operations  1.29 us (3%)
    pallas_call x1, Pallas kernels, local(): pl.pallas_call(functools.partial(kernel, scale, owners), out_shape=(jax.S...  37.6 us
    pallas_call x1, Pallas kernels, finish(): pl.pallas_call(place, out_shape=tuple((jax.ShapeDtypeStruct(a.shape, a.dt...  0.9 us

profile of v6, /device:TPU:0, one launch (start us, length us, event | category | flops | bytes accessed | tf_op | source)
XLA Modules:
  0.0 39.8 jit_solution(6086963327248735317)
XLA Ops:
  1.3 37.6 %shard_map.103 = (bf16[512,256]{1,0:T(8,128)(2,1)S(1)}, bf16[4,128,256]{2,1,0:T(8,128)(2,1)S(1)}, f32[256,256]{1,0:T(8,128)S(1)}) custom-call(s32[40]{0:T(128)} %rows_hbm.1, s32[40]{0:T(128)} %cols_hbm.1, s32[1]{0:T(128)S(6)} %copy.11.count_s, s32[16]{0:T(128)} %bitcast.5, bf16[4,128,256]{2,1,0:T(8,128)(2,1)} %bitcast.4, bf16[256,256]{1,0:T(8,128)(2,1)} %weight_hbm.1, ...), custom_call_target="tpu_custom_call" | custom-call | tf_op jit(solution)/shard_map/pallas_call | solution.py:518
  38.9 0.9 %shard_map.104 = (bf16[512,256]{1,0:T(8,128)(2,1)}, bf16[512,256]{1,0:T(8,128)(2,1)}, f32[256,256]{1,0:T(8,128)}) custom-call(bf16[512,256]{1,0:T(8,128)(2,1)S(1)} %get-tuple-element.6.refs_0_, bf16[512,256]{1,0:T(8,128)(2,1)S(1)} %bitcast.3, f32[256,256]{1,0:T(8,128)S(1)} %get-tuple-element.8.refs_2_), custom_call_target="tpu_custom_call" | custom-call | tf_op jit(solution)/shard_map/pallas_call | solution.py:487

commit v7 on v6

--- a/solution.py
+++ b/solution.py
@@ -369,7 +369,7 @@
 
     flat = 2 * me + col
     keep_own = jnp.where(is_owner, mine, doms)
-    others(doms, lax.rem(me, doms), keep_own,
+    others(doms, lax.rem(me + doms // 2, doms), keep_own,
            lambda i: remote(wchunk.at[i], wpart.at[flat], r_send, r_recv, first + i, 1).start())
 
     for j in range(half):

time: 39.9 us -> 39.8 us (level)
  no operation moved by 1% of the time
where the time goes in v7:
time: 39.8 us; the launch traced here: 39.7 us
  Pallas kernels  38.4 us (96%)
  between operations  1.29 us (3%)
    pallas_call x1, Pallas kernels, local(): pl.pallas_call(functools.partial(kernel, scale, owners), out_shape=(jax.S...  37.5 us
    pallas_call x1, Pallas kernels, finish(): pl.pallas_call(place, out_shape=tuple((jax.ShapeDtypeStruct(a.shape, a.dt...  0.9 us

profile of v7, /device:TPU:0, one launch (start us, length us, event | category | flops | bytes accessed | tf_op | source)
XLA Modules:
  0.0 39.7 jit_solution(10523784294552893179)
XLA Ops:
  1.3 37.5 %shard_map.103 = (bf16[512,256]{1,0:T(8,128)(2,1)S(1)}, bf16[4,128,256]{2,1,0:T(8,128)(2,1)S(1)}, f32[256,256]{1,0:T(8,128)S(1)}) custom-call(s32[40]{0:T(128)} %rows_hbm.1, s32[40]{0:T(128)} %cols_hbm.1, s32[1]{0:T(128)S(6)} %copy.11.count_s, s32[16]{0:T(128)} %bitcast.5, bf16[4,128,256]{2,1,0:T(8,128)(2,1)} %bitcast.4, bf16[256,256]{1,0:T(8,128)(2,1)} %weight_hbm.1, ...), custom_call_target="tpu_custom_call" | custom-call | tf_op jit(solution)/shard_map/pallas_call | solution.py:518
  38.8 0.9 %shard_map.104 = (bf16[512,256]{1,0:T(8,128)(2,1)}, bf16[512,256]{1,0:T(8,128)(2,1)}, f32[256,256]{1,0:T(8,128)}) custom-call(bf16[512,256]{1,0:T(8,128)(2,1)S(1)} %get-tuple-element.6.refs_0_, bf16[512,256]{1,0:T(8,128)(2,1)S(1)} %bitcast.3, f32[256,256]{1,0:T(8,128)S(1)} %get-tuple-element.8.refs_2_), custom_call_target="tpu_custom_call" | custom-call | tf_op jit(solution)/shard_map/pallas_call | solution.py:487
